TPU v7x, 128 devices: a whole 4x4x4 slice. The times are simulated.
128 devices in a mesh: row: 8 (over y, core), col: 4 (over z), mp: 4 (over x).
Axes of the slice: x: 4, y: 4, z: 4, core: 2. Of those that a mesh axis runs over, the one named last changes fastest.
Arguments:
- hidden: bfloat16 [32768, 3584], P(('row', 'col'), 'mp'), may hold values from -6 to 6
- old_logp: float32 [32768], P(('row', 'col')), may hold values from -0.6 to 0.6
- rewards: float32 [256], P(('row', 'col')), may hold values from -4 to 4
- resp_dest: int32 [256], P(('row', 'col')), may hold values from 0 to 31, as said below
- resp_len: int32 [256], P(('row', 'col')), may hold values from 1 to 128, as said below
- resp_offset: int32 [256], P(('row', 'col')), may hold values from 0 to 511, as said below
- prompt_group: int32 [256], P(('row', 'col')), may hold values from 0 to 31, as said below
- attn_gain: bfloat16 [3584], replicated, may hold values from 0.099609375 to 1.8984375
- w_query: bfloat16 [3584, 3584], P(None, 'mp'), may hold values from -0.09375 to 0.09375
- q_bias: bfloat16 [3584], P('mp'), may hold values from -3 to 3
- w_key: bfloat16 [3584, 512], P(None, 'mp'), may hold values from -0.09375 to 0.09375
- k_bias: bfloat16 [512], P('mp'), may hold values from -6 to 6
- w_value: bfloat16 [3584, 512], P(None, 'mp'), may hold values from -0.09375 to 0.09375
- v_bias: bfloat16 [512], P('mp'), may hold values from -3 to 3
- w_out: bfloat16 [3584, 3584], P('mp'), may hold values from -0.5 to 0.5
- final_gain: bfloat16 [3584], replicated, may hold values from 0.099609375 to 1.8984375
- chosen_rows: bfloat16 [16384, 3584], P(('row', 'col', 'mp')), may hold values from -0.01171875 to 0.01171875
- log_normalizer: float32 [16384], P(('row', 'col', 'mp')), may hold values from -0.6 to 0.6
Outputs:
- objective: float32 [16384], P(('row', 'col', 'mp'))
- loss: float32 [], replicated
Inputs may be any that keep to these rules, and one draw needn't show every extreme that they name: `resp_dest`: ranks are numbered row index * 4 + col index. A rank's responses go to ranks of the same col index: exactly 1 of them to each such rank, itself included; so every rank receives exactly 8 responses. `resp_len`: the responses bound for one rank hold at most 512 tokens together; in every draw some rank's responses fill all 512 positions, and some response has exactly 128. `resp_offset`: responses bound for one rank lie end to end from position 0, without gaps or intersection. `prompt_group`: each of the 32 groups has exactly 8 responses.
All inputs are finite; a program needn't handle non-finite values.
Results may differ from a plain program's by a relative error of at most 0.0019.
Values may be sent and summed in bfloat16 or wider, within the bound.
No kernel may reach another device: no remote copies, remote signals or barrier semaphores. Data moves between devices by JAX's collectives and lax.ppermute only.
A program may use at most 128 MiB of HBM per device.

v0:
```python
import jax
import jax.numpy as jnp
from jax import lax
from jax.sharding import Mesh
from jax.sharding import PartitionSpec as P

HEAD = 128
GROUP_SIZE = 8
ROW = ("row_0", "row_1")
ROW_COL = ("row_0", "row_1", "col")
ROW_COL_MP = ("row_0", "row_1", "col", "mp")


norm_eps = 1e-06
rope_theta = 1000000.0
clip_low = 0.2
clip_high = 0.28
std_floor = 1.0
mask_fill = -1e30


def sent_to_all(value, axis):
    copies = jnp.broadcast_to(value, (lax.axis_size(axis), *value.shape))
    return lax.all_to_all(copies, axis, split_axis=0, concat_axis=0, tiled=True)


def of_everyone(value, axis):
    everything = sent_to_all(value, axis)
    return jnp.sum(everything, axis=0)


def together(arrays, axis):
    ends = [0]
    for a in arrays:
        ends.append(ends[-1] + a.size)
    total = of_everyone(jnp.concatenate([a.ravel() for a in arrays]), axis)
    return tuple((total[b:e].reshape(a.shape) for a, b, e in zip(arrays, ends, ends[1:])))


def over_axes(value, axes):
    for axis in axes:
        value = lax.psum(value, axis)
    return value


def rotary(matrix, positions):
    half_size = matrix.shape[-1] // 2
    exponents = jnp.arange(half_size, dtype=jnp.float32) * (2.0 / matrix.shape[-1])
    frequency = rope_theta ** (-exponents)
    angles = positions[:, None] * frequency[None, :]
    cosine_table = jnp.cos(angles)[:, None, :]
    sine_table = jnp.sin(angles)[:, None, :]
    first_half = matrix[..., :half_size]
    second_half = matrix[..., half_size:]
    return jnp.concatenate(
        [
            first_half * cosine_table - second_half * sine_table,
            second_half * cosine_table + first_half * sine_table,
        ],
        -1,
    )


def body(
    hidden,
    old_logp,
    rewards,
    resp_dest,
    resp_len,
    resp_offset,
    prompt_group,
    attn_gain,
    w_query,
    q_bias,
    w_key,
    k_bias,
    w_value,
    v_bias,
    w_out,
    final_gain,
    chosen_rows,
    log_normalizer,
):
    highest = lax.Precision.HIGHEST
    row_ranks = lax.axis_size(ROW)
    col_ranks = lax.axis_size("col")
    rank_count = row_ranks * col_ranks
    response_count = resp_dest.shape[0]
    per_peer = response_count // row_ranks
    group_count = rank_count * response_count // GROUP_SIZE
    slot_length = hidden.shape[0] // response_count
    feature_count = hidden.shape[1]
    pack_length = response_count * slot_length // 2
    shard_count = lax.axis_size("mp")
    row_count = pack_length // shard_count
    slot_iota = jnp.arange(response_count, dtype=jnp.int32)
    group_iota = jnp.arange(group_count, dtype=jnp.int32)
    dest_row = resp_dest // col_ranks
    earlier = (slot_iota[None, :] < slot_iota[:, None]) & (dest_row[None, :] == dest_row[:, None])
    slot_in_peer = jnp.sum(earlier.astype(jnp.int32), 1)
    send_slot = dest_row * per_peer + slot_in_peer
    selector = send_slot[None, :] == slot_iota[:, None]
    selector_wide = selector.astype(jnp.float32)
    send_rows = jnp.dot(
        selector.astype(jnp.bfloat16),
        hidden.reshape(response_count, slot_length * feature_count),
        preferred_element_type=jnp.float32,
    ).astype(jnp.bfloat16)
    send_rows = send_rows.reshape(row_ranks, per_peer * slot_length, feature_count)
    send_logp = jnp.dot(
        selector_wide, old_logp.reshape(response_count, slot_length), precision=highest
    )
    send_length = jnp.dot(selector_wide, resp_len.astype(jnp.float32), precision=highest)
    send_offset = jnp.dot(selector_wide, resp_offset.astype(jnp.float32), precision=highest)
    member = (prompt_group[:, None] == group_iota[None, :]).astype(jnp.float32)
    send_info = jnp.stack(
        [
            send_length,
            send_offset,
            jnp.dot(selector_wide, rewards, precision=highest),
            jnp.dot(selector_wide, prompt_group.astype(jnp.float32), precision=highest),
        ],
        1,
    )
    send_info = send_info.reshape(row_ranks, per_peer, send_info.shape[1])
    recv_rows = lax.all_to_all(send_rows, ROW, split_axis=0, concat_axis=0, tiled=True)
    recv_logp, recv_info = (
        lax.all_to_all(send_logp, ROW, split_axis=0, concat_axis=0, tiled=True),
        lax.all_to_all(send_info, ROW, split_axis=0, concat_axis=0, tiled=True),
    )
    recv_info = recv_info.reshape(response_count, recv_info.shape[2])
    lengths = recv_info[:, 0].astype(jnp.int32)
    offsets = recv_info[:, 1].astype(jnp.int32)
    slots = jnp.arange(pack_length, dtype=jnp.int32)[:, None]
    covered = (slots >= offsets[None, :]) & (slots < (offsets + lengths)[None, :])
    occupied = jnp.any(covered, 1)
    within_all = slots - offsets[None, :]
    token_index = jnp.sum(jnp.where(covered, slot_iota[None, :] * slot_length + within_all, 0), 1)
    positions = jnp.sum(jnp.where(covered, within_all, 0), 1).astype(jnp.float32)
    segment = jnp.where(occupied, jnp.sum(jnp.where(covered, slot_iota[None, :], 0), 1), -1)
    flat_rows = recv_rows.reshape(-1, feature_count)
    packed = jnp.where(occupied[:, None], flat_rows[token_index], jnp.zeros((), jnp.bfloat16))
    gathered = lax.all_gather(packed, "mp", axis=1, tiled=True)
    inverse = lax.rsqrt(
        jnp.mean(jnp.square(gathered.astype(jnp.float32)), -1, keepdims=True) + norm_eps
    )
    normed = (gathered.astype(jnp.float32) * inverse * attn_gain.astype(jnp.float32)).astype(
        jnp.bfloat16
    )
    heads_local = w_query.shape[1] // HEAD
    key_heads = w_key.shape[1] // HEAD
    queries = jnp.dot(normed, w_query, preferred_element_type=jnp.float32) + q_bias.astype(
        jnp.float32
    )
    queries = rotary(queries.reshape(pack_length, heads_local, HEAD), positions).astype(
        jnp.bfloat16
    )
    key_rows = jnp.dot(normed, w_key, preferred_element_type=jnp.float32) + k_bias.astype(
        jnp.float32
    )
    key_rows = rotary(key_rows.reshape(pack_length, key_heads, HEAD), positions).astype(
        jnp.bfloat16
    )
    value_rows = (
        (jnp.dot(normed, w_value, preferred_element_type=jnp.float32) + v_bias.astype(jnp.float32))
        .astype(jnp.bfloat16)
        .reshape(pack_length, key_heads, HEAD)
    )
    grouped = queries.reshape(pack_length, key_heads, heads_local // key_heads, HEAD)
    block_size = min(512, pack_length)
    scores = jnp.einsum(
        "qkgd,ekd->kgqe", grouped, key_rows, preferred_element_type=jnp.float32
    ) * HEAD ** (-0.5)
    allowed = (segment[0:block_size, None] == segment[None, :block_size]) & (
        jnp.arange(block_size)[None, :] <= jnp.arange(0, block_size)[:, None]
    )
    scores = jnp.where(allowed, scores, mask_fill)
    highest_score = jnp.max(scores, -1, keepdims=True)
    exponent = jnp.exp(scores - highest_score)
    weights = (exponent / jnp.sum(exponent, -1, keepdims=True)).astype(jnp.bfloat16)
    block_out = jnp.einsum(
        "kgqe,ekd->qkgd", weights, value_rows, preferred_element_type=jnp.float32
    )
    pieces = block_out.reshape(block_size, heads_local * HEAD).astype(jnp.bfloat16)
    branch = lax.psum_scatter(
        jnp.dot(pieces, w_out, preferred_element_type=jnp.float32).astype(jnp.bfloat16),
        "mp",
        scatter_dimension=0,
        tiled=True,
    ).astype(jnp.float32)
    own_start = lax.axis_index("mp") * row_count
    residual = lax.dynamic_slice_in_dim(gathered, own_start, row_count, 0)
    residual_out = (residual.astype(jnp.float32) + branch).astype(jnp.bfloat16)
    final_rows = residual_out.astype(jnp.float32)
    final_inverse = lax.rsqrt(jnp.mean(final_rows * final_rows, -1, keepdims=True) + norm_eps)
    logits = jnp.sum(
        final_rows
        * final_inverse
        * final_gain.astype(jnp.float32)
        * chosen_rows.astype(jnp.float32),
        -1,
    )
    own_covered = lax.dynamic_slice_in_dim(covered, own_start, row_count, 0)
    own_occupied = lax.dynamic_slice_in_dim(occupied, own_start, row_count, 0)
    own_token = lax.dynamic_slice_in_dim(token_index, own_start, row_count, 0)
    own_old = jnp.where(own_occupied, recv_logp.reshape(-1)[own_token], 0.0)
    totals, squares = together(
        (
            jnp.dot(rewards, member, precision=highest),
            jnp.dot(rewards * rewards, member, precision=highest),
        ),
        ROW_COL,
    )
    means = totals / GROUP_SIZE
    variance = jnp.maximum(squares / GROUP_SIZE - means * means, 0.0)
    means, scales = (means, jnp.maximum(jnp.sqrt(variance), std_floor))
    pair_member = (recv_info[:, 3].astype(jnp.int32)[:, None] == group_iota[None, :]).astype(
        jnp.float32
    )
    pair_adv = (recv_info[:, 2] - jnp.dot(pair_member, means, precision=highest)) / jnp.dot(
        pair_member, scales, precision=highest
    )
    token_adv = jnp.sum(jnp.where(own_covered, pair_adv[None, :], 0.0), 1)
    ratios = jnp.exp(logits - log_normalizer - own_old)
    bounded = jnp.clip(ratios, 1.0 - clip_low, 1.0 + clip_high)
    objective = jnp.where(own_occupied, jnp.minimum(ratios * token_adv, bounded * token_adv), 0.0)
    loss_sum, counted = (
        over_axes(jnp.sum(objective), ROW_COL_MP),
        over_axes(jnp.sum(own_occupied.astype(jnp.float32)), ROW_COL_MP),
    )
    return (objective, -loss_sum / counted)


def solution(mesh):
    finer = Mesh(
        mesh.devices.reshape(4, 2, mesh.shape["col"], mesh.shape["mp"]),
        ("row_0", "row_1", "col", "mp"),
    )
    placed = (
        P(ROW_COL, "mp"),
        P(ROW_COL),
        P(ROW_COL),
        P(ROW_COL),
        P(ROW_COL),
        P(ROW_COL),
        P(ROW_COL),
        P(),
        P(None, "mp"),
        P("mp"),
        P(None, "mp"),
        P("mp"),
        P(None, "mp"),
        P("mp"),
        P("mp", None),
        P(),
        P(ROW_COL_MP, None),
        P(ROW_COL_MP),
    )
    return jax.shard_map(
        body, mesh=finer, in_specs=placed, out_specs=(P(ROW_COL_MP), P()), check_vma=False
    )
```

profile of v0, /device:TPU:0, one launch (start us, length us, event | category | flops | bytes accessed | tf_op | source)
XLA Modules:
  0.0 239.6 jit_solution(6732604042234698789)
XLA Ops:
  12.6 4.6 %all-to-all-start = ((f32[8,1,4]{2,1,0:T(1,128)}), f32[8,1,4]{2,1,0:T(1,128)S(1)}, u32[]{:S(2)}, u32[]{:S(2)}) async-start(f32[8,1,4]{2,1,0:T(1,128)} %copy.51), calls=%async_computation | async-start | bytes 8192 | tf_op jit(solution)/shard_map/all_to_all | solution.py:129
  17.2 2.3 reshape.258
  22.5 4.0 %all-to-all-start.1 = ((bf16[8,128,896]{2,1,0:T(8,128)(2,1)}), bf16[8,128,896]{2,1,0:T(8,128)(2,1)S(1)}, u32[]{:S(2)}, u32[]{:S(2)}) async-start(bf16[8,128,896]{2,1,0:T(8,128)(2,1)} %copy.53), calls=%async_computation.1 | async-start | bytes 3670016 | tf_op jit(solution)/shard_map/all_to_all | solution.py:126
  28.0 22.9 %all-to-all-done.1 = bf16[8,128,896]{2,1,0:T(8,128)(2,1)S(1)} async-done(((bf16[8,128,896]{2,1,0:T(8,128)(2,1)}), bf16[8,128,896]{2,1,0:T(8,128)(2,1)S(1)}, u32[]{:S(2)}, u32[]{:S(2)}) %all-to-all-start.1) | async-done | bytes 1835040 | tf_op jit(solution)/shard_map/all_to_all | solution.py:126
  50.9 2.8 %gather_fusion = bf16[512,896]{1,0:T(8,128)(2,1)} fusion(bf16[1024,896]{1,0:T(8,128)(2,1)S(1)} %bitcast.121, s32[1024]{0:T(1024)S(1)} %pad_clamp_fusion.1), kind=kCustom, calls=%fused_computation | custom fusion | bytes 1837056 | tf_op jit(solution)/shard_map/gather | solution.py:142
  53.6 2.3 broadcast_select_fusion
  58.4 41.8 %all-gather.2.cloned.1.call-done = bf16[512,3584]{1,0:T(8,128)(2,1)} async-done(((bf16[512,896]{1,0:T(8,128)(2,1)}), bf16[512,3584]{1,0:T(8,128)(2,1)}) %all-gather.2.cloned.1.call-update) | async-done | bytes 3670032 | tf_op jit(solution)/shard_map/all_gather | solution.py:143
  100.3 3.0 %fusion = f32[512]{0:T(512)S(1)} fusion(bf16[512,3584]{1,0:T(8,128)(2,1)} %all-gather.2.cloned.1.call-done), kind=kLoop, calls=%fused_computation.5 | loop fusion | flops 5504512 | bytes 3672064 | tf_op jit(solution)/shard_map/reduce_sum | solution.py:145
  103.9 8.1 %convolution_add_fusion = f32[512,896]{1,0:T(8,128)} fusion(bf16[3584,896]{1,0:T(8,128)(2,1)} %param.26, f32[896]{0:T(1024)S(1)} %convert_element_type.138, bf16[512,3584]{1,0:T(8,128)(2,1)S(1)} %copy-done.2, f32[3584]{0:T(1024)S(1)} %convert_element_type.132, f32[512]{0:T(512)S(1)} %add_rsqrt_fusion), kind=kOutput, calls=%fused_computation.26 | convolution fusion | flops 3296133120 | bytes 11947520 | tf_op jit(solution)/shard_map/dot_general | solution.py:152
  116.9 3.0 %copy.68 = f32[512,7,64]{2,0,1:T(8,128)} copy(f32[512,7,64]{0,2,1:T(8,128)} %get-tuple-element.17) | data formatting | bytes 1835008
  119.9 3.9 %fusion.15 = f32[512,1,128]{0,2,1:T(8,128)S(1)} fusion(bf16[3584,128]{1,0:T(8,128)(2,1)} %param.28, f32[128]{0:T(128)} %convert_element_type.136, bf16[512,3584]{1,0:T(8,128)(2,1)} %all-gather.2.cloned.1.call-done, f32[3584]{0:T(1024)} %copy-done.5, f32[512]{0:T(512)} %copy-done.13), kind=kOutput, calls=%fused_computation.29 | convolution fusion | flops 477167616 | bytes 4866560 | tf_op jit(solution)/shard_map/dot_general | solution.py:158
  127.0 3.0 %copy-done.1 = f32[512,512,7]{1,0,2:T(8,128)} copy-done((f32[512,512,7]{1,0,2:T(8,128)}, f32[512,512,7]{1,0,2:T(8,128)S(1)}, u32[]{:S(2)}) %copy-start.1) | copy-done | bytes 7340056
  131.6 7.6 %fusion.12 = bf16[128,7,512]{2,0,1:T(8,128)(2,1)S(1)} fusion(f32[7,512]{1,0:T(8,128)S(1)} %fusion.3, f32[7,512]{1,0:T(8,128)S(1)} %get-tuple-element.28, f32[512,512,7]{1,0,2:T(8,128)} %copy-done.1, pred[512,512]{0,1:T(8,128)(4,1)S(1)} %fusion.20, bf16[3584,128]{1,0:T(8,128)(2,1)S(1)} %copy-done, f32[128]{0:T(128)S(1)} %copy-done.23, ...), kind=kOutput, calls=%fused_computation.27 | convolution fusion | flops 956628992 | bytes 13152768 | tf_op jit(solution)/shard_map/kgqe,ekd->qkgd/dot_general | solution.py:181
  139.2 8.3 %convolution_convert_fusion.1 = bf16[512,3584]{1,0:T(8,128)(2,1)} fusion(bf16[512,896]{0,1:T(8,128)(2,1)S(1)} %bitcast.130, bf16[896,3584]{1,0:T(8,128)(2,1)} %param.32), kind=kOutput, calls=%fused_computation.12 | convolution fusion | flops 3290169344 | bytes 11010048 | tf_op jit(solution)/shard_map/dot_general | solution.py:186
  148.9 4.3 %all-to-all-start.2 = ((f32[8,1,128]{2,1,0:T(1,128)}), f32[8,1,128]{2,1,0:T(1,128)S(1)}, u32[]{:S(2)}, u32[]{:S(2)}) async-start(f32[8,1,128]{2,1,0:T(1,128)} %bitcast.34), calls=%async_computation.3 | async-start | bytes 8192 | tf_op jit(solution)/shard_map/all_to_all | solution.py:128
  153.7 4.7 %all-to-all-done.2 = f32[8,1,128]{2,1,0:T(1,128)S(1)} async-done(((f32[8,1,128]{2,1,0:T(1,128)}), f32[8,1,128]{2,1,0:T(1,128)S(1)}, u32[]{:S(2)}, u32[]{:S(2)}) %all-to-all-start.2) | async-done | bytes 4128 | tf_op jit(solution)/shard_map/all_to_all | solution.py:128
  159.0 5.4 %all-to-all-start.3 = ((f32[32,1,64]{2,1,0:T(1,128)}), f32[32,1,64]{2,1,0:T(1,128)S(1)}, u32[]{:S(2)}, u32[]{:S(2)}) async-start(f32[32,1,64]{2,1,0:T(1,128)} %broadcast_in_dim.65), calls=%async_computation.4 | async-start | bytes 32768 | tf_op jit(solution)/shard_map/all_to_all | solution.py:24
  165.5 6.4 %all-to-all-done.3 = f32[32,1,64]{2,1,0:T(1,128)S(1)} async-done(((f32[32,1,64]{2,1,0:T(1,128)}), f32[32,1,64]{2,1,0:T(1,128)S(1)}, u32[]{:S(2)}, u32[]{:S(2)}) %all-to-all-start.3) | async-done | bytes 8224 | tf_op jit(solution)/shard_map/all_to_all | solution.py:24
  173.0 17.5 %reduce-scatter.2.cloned.1.call-done = bf16[128,3584]{1,0:T(8,128)(2,1)} async-done(((bf16[512,3584]{1,0:T(8,128)(2,1)}), bf16[128,3584]{1,0:T(8,128)(2,1)}) %reduce-scatter.2.cloned.1.call-update) | async-done | bytes 917520 | tf_op jit(solution)/shard_map/reduce_scatter | solution.py:185
  192.3 2.1 fusion.11
  195.6 11.2 %all-reduce.2 = (f32[]{:T(128)}, f32[]{:T(128)}) all-reduce(f32[]{:T(128)} %get-tuple-element.13, f32[]{:T(128)} %get-tuple-element.27), channel_id=1, replica_groups=mesh['row_0'=4,'row_1'=2,'col'=4,'mp'=4] {'row_0'}, use_global_device_ids=true, to_apply=%region_14.15 | all-reduce | flops 2 | bytes 16 | tf_op jit(solution)/shard_map/psum | solution.py:42
  206.8 3.1 %all-reduce.3 = (f32[]{:T(128)}, f32[]{:T(128)}) all-reduce(f32[]{:T(128)} %get-tuple-element.9, f32[]{:T(128)} %get-tuple-element.10), channel_id=1, replica_groups=mesh['row_0'=4,'row_1'=2,'col'=4,'mp'=4] {'row_1'}, use_global_device_ids=true, to_apply=%region_15.16 | all-reduce | flops 2 | bytes 16 | tf_op jit(solution)/shard_map/psum | solution.py:42
  209.9 11.3 %all-reduce.1 = (f32[]{:T(128)}, f32[]{:T(128)}) all-reduce(f32[]{:T(128)} %get-tuple-element.11, f32[]{:T(128)} %get-tuple-element.12), channel_id=1, replica_groups=mesh['row_0'=4,'row_1'=2,'col'=4,'mp'=4] {'col'}, use_global_device_ids=true, to_apply=%region_16.17 | all-reduce | flops 2 | bytes 16 | tf_op jit(solution)/shard_map/psum | solution.py:42
  221.2 9.2 %all-reduce = (f32[]{:T(128)}, f32[]{:T(128)}) all-reduce(f32[]{:T(128)} %get-tuple-element.7, f32[]{:T(128)} %get-tuple-element.8), channel_id=1, replica_groups=mesh['row_0'=4,'row_1'=2,'col'=4,'mp'=4] {'mp'}, use_global_device_ids=true, to_apply=%region_17.18 | all-reduce | flops 2 | bytes 16 | tf_op jit(solution)/shard_map/psum | solution.py:42
  (103 shorter events, 30.2 us)
Async XLA Ops:
  7.2 124.4 %copy-start = (bf16[3584,128]{1,0:T(8,128)(2,1)S(1)}, bf16[3584,128]{1,0:T(8,128)(2,1)}, u32[]{:S(2)}) copy-start(bf16[3584,128]{1,0:T(8,128)(2,1)} %param.30) | copy-start | bytes 2752516
  8.8 11.4 %copy-start.15 = (s32[8]{0:T(128)}, s32[8]{0:T(128)S(1)}, u32[]{:S(2)}) copy-start(s32[8]{0:T(128)S(1)} %fusion.84) | copy-start | bytes 100
  12.6 9.9 %all-to-all-start = ((f32[8,1,4]{2,1,0:T(1,128)}), f32[8,1,4]{2,1,0:T(1,128)S(1)}, u32[]{:S(2)}, u32[]{:S(2)}) async-start(f32[8,1,4]{2,1,0:T(1,128)} %copy.51), calls=%async_computation | async-start | bytes 8192 | tf_op jit(solution)/shard_map/all_to_all | solution.py:129
  22.5 28.4 %all-to-all-start.1 = ((bf16[8,128,896]{2,1,0:T(8,128)(2,1)}), bf16[8,128,896]{2,1,0:T(8,128)(2,1)S(1)}, u32[]{:S(2)}, u32[]{:S(2)}) async-start(bf16[8,128,896]{2,1,0:T(8,128)(2,1)} %copy.53), calls=%async_computation.1 | async-start | bytes 3670016 | tf_op jit(solution)/shard_map/all_to_all | solution.py:126
  26.5 73.8 %all-gather.2.cloned.1.call-start = ((), (), s32[]{:S(2)}) async-start(), calls=%async_computation.5 | async-start | bytes 4587520 | tf_op jit(solution)/shard_map/all_gather | solution.py:143
  50.9 5.1 %copy-start.7 = (bf16[3584]{0:T(1024)(128)(2,1)S(1)}, bf16[3584]{0:T(1024)(128)(2,1)}, u32[]{:S(2)}) copy-start(bf16[3584]{0:T(1024)(128)(2,1)} %param.25) | copy-start | bytes 21508
  50.9 5.1 %copy-start.12 = (bf16[896]{0:T(1024)(128)(2,1)S(1)}, bf16[896]{0:T(1024)(128)(2,1)}, u32[]{:S(2)}) copy-start(bf16[896]{0:T(1024)(128)(2,1)} %param.27) | copy-start | bytes 5380
  50.9 5.2 %copy-start.19 = (bf16[128]{0:T(256)(128)(2,1)S(1)}, bf16[128]{0:T(256)(128)(2,1)}, u32[]{:S(2)}) copy-start(bf16[128]{0:T(256)(128)(2,1)} %param.29) | copy-start | bytes 772
  50.9 5.8 %copy-start.20 = (bf16[128]{0:T(256)(128)(2,1)S(1)}, bf16[128]{0:T(256)(128)(2,1)}, u32[]{:S(2)}) copy-start(bf16[128]{0:T(256)(128)(2,1)} %param.31) | copy-start | bytes 772
  55.9 134.5 %reduce-scatter.2.cloned.1.call-start = ((), (), s32[]{:S(2)}) async-start(), calls=%async_computation.6 | async-start | bytes 4587520 | tf_op jit(solution)/shard_map/reduce_scatter | solution.py:185
  56.0 47.2 %copy-start.5 = (f32[3584]{0:T(1024)}, f32[3584]{0:T(1024)S(1)}, u32[]{:S(2)}) copy-start(f32[3584]{0:T(1024)S(1)} %convert_element_type.132) | copy-start | bytes 43012
  100.3 3.6 %copy-start.2 = (bf16[512,3584]{1,0:T(8,128)(2,1)S(1)}, bf16[512,3584]{1,0:T(8,128)(2,1)}, u32[]{:S(2)}) copy-start(bf16[512,3584]{1,0:T(8,128)(2,1)} %all-gather.2.cloned.1.call-done) | copy-start | bytes 11010052
  119.9 3.9 %copy-start.11 = (f32[64]{0:T(128)S(1)}, f32[64]{0:T(128)}, u32[]{:S(2)}) copy-start(f32[64]{0:T(128)} %copy-done.10) | copy-start | bytes 772
  119.9 4.5 %copy-start.3 = (f32[512,7,64]{2,0,1:T(8,128)S(1)}, f32[512,7,64]{2,0,1:T(8,128)}, u32[]{:S(2)}) copy-start(f32[512,7,64]{2,0,1:T(8,128)} %copy.68) | copy-start | bytes 2752516
  127.0 3.0 %copy-start.1 = (f32[512,512,7]{1,0,2:T(8,128)}, f32[512,512,7]{1,0,2:T(8,128)S(1)}, u32[]{:S(2)}) copy-start(f32[512,512,7]{1,0,2:T(8,128)S(1)} %get-tuple-element.29) | copy-start | bytes 22020100
  130.0 1.6 copy-start.23
  147.5 5.7 %copy-start.8 = (bf16[3584]{0:T(1024)(128)(2,1)S(1)}, bf16[3584]{0:T(1024)(128)(2,1)}, u32[]{:S(2)}) copy-start(bf16[3584]{0:T(1024)(128)(2,1)} %param.33) | copy-start | bytes 21508
  147.5 5.7 %copy-start.21 = (s32[8]{0:T(128)S(1)}, s32[8]{0:T(128)}, u32[]{:S(2)}) copy-start(s32[8]{0:T(128)} %param.24) | copy-start | bytes 100
  147.5 5.7 %copy-start.22 = (f32[8]{0:T(128)S(1)}, f32[8]{0:T(128)}, u32[]{:S(2)}) copy-start(f32[8]{0:T(128)} %param.20) | copy-start | bytes 100
  147.5 24.4 %copy-start.18 = (s32[8]{0:T(128)S(1)}, s32[8]{0:T(128)}, u32[]{:S(2)}) copy-start(s32[8]{0:T(128)} %get-tuple-element.23) | copy-start | bytes 100
  147.5 44.8 %copy-start.4 = (bf16[128,3584]{1,0:T(8,128)(2,1)S(1)}, bf16[128,3584]{1,0:T(8,128)(2,1)}, u32[]{:S(2)}) copy-start(bf16[128,3584]{1,0:T(8,128)(2,1)} %param.34) | copy-start | bytes 2752516
  148.1 46.3 %copy-start.17 = (f32[128]{0:T(128)S(1)}, f32[128]{0:T(128)}, u32[]{:S(2)}) copy-start(f32[128]{0:T(128)} %param.35) | copy-start | bytes 1540
  148.9 9.6 %all-to-all-start.2 = ((f32[8,1,128]{2,1,0:T(1,128)}), f32[8,1,128]{2,1,0:T(1,128)S(1)}, u32[]{:S(2)}, u32[]{:S(2)}) async-start(f32[8,1,128]{2,1,0:T(1,128)} %bitcast.34), calls=%async_computation.3 | async-start | bytes 8192 | tf_op jit(solution)/shard_map/all_to_all | solution.py:128
  159.0 12.8 %all-to-all-start.3 = ((f32[32,1,64]{2,1,0:T(1,128)}), f32[32,1,64]{2,1,0:T(1,128)S(1)}, u32[]{:S(2)}, u32[]{:S(2)}) async-start(f32[32,1,64]{2,1,0:T(1,128)} %broadcast_in_dim.65), calls=%async_computation.4 | async-start | bytes 32768 | tf_op jit(solution)/shard_map/all_to_all | solution.py:24
  (6 other events, 6.4 us)
Sparse Core Ops, SparseCore 0:
  56.1 44.1 all-gather.1
  147.7 42.7 reduce-scatter.1
where the time goes:
time: 240 us
  waiting for transfers between devices  94.2 us (39%)
  matrix products  35.1 us (15%)
  blocking collectives  34.8 us (14%)
  local copies, waits for them, and re-layouts  21.2 us (9%)
  other arithmetic  19.2 us (8%)
  starting transfers between devices  18.4 us (8%)
  between operations  16.8 us (7%)
    all_gather x1, waiting for transfers between devices, body(): gathered = lax.all_gather(packed, 'mp', axis=1, tiled=True)  41.8 us
    psum x4, blocking collectives, over_axes(): value = lax.psum(value, axis)  34.8 us
    all_to_all x1, waiting for transfers between devices, body(): lax.all_to_all(send_rows, ROW, split_axis=0, concat_axis=0, tiled=True)  22.9 us
    reduce_scatter x1, waiting for transfers between devices, body(): lax.psum_scatter(jnp.dot(pieces, w_out, preferred_element_type=jnp.float3...  17.5 us
    unnamed x50, local copies, waits for them, and re-layouts  8.94 us
    dot_general x1, matrix products, body(): jnp.dot(pieces, w_out, preferred_element_type=jnp.float32)  8.28 us
    dot_general x1, matrix products, body(): jnp.dot(normed, w_query, preferred_element_type=jnp.float32)  8.08 us
    dot_general x1, matrix products, body(): jnp.einsum('kgqe,ekd->qkgd', weights, value_rows, preferred_element_type=...  7.58 us
  transfers between devices with their start and end apart: 6, of which 6 were waited for; matrix products, arithmetic and copies ran while one was open for 5% of the time, Pallas kernels for 0%

commit v1 on v0

v1 whole, which is shorter than its diff:
```python
import functools

import jax
import jax.numpy as jnp
from jax import lax
from jax.experimental import pallas as pl
from jax.experimental.pallas import tpu as pltpu
from jax.sharding import PartitionSpec as P


HEAD = 128
GROUP_SIZE = 8
SLOT = 128
ROWS = 8
COLS = 4
SHARDS = 4
PACK = 512
ROW_COL = ("row", "col")
ROW_COL_MP = ("row", "col", "mp")
CHUNKS = (384, 512)
STARTS = (0, 384)

norm_eps = 1e-06
rope_theta = 1000000.0
clip_low = 0.2
clip_high = 0.28
std_floor = 1.0
mask_fill = -1e30

F32 = jnp.float32
BF16 = jnp.bfloat16
VMEM = pl.BlockSpec(memory_space=pltpu.VMEM)
SMEM = pl.BlockSpec(memory_space=pltpu.SMEM)
HBM = pl.BlockSpec(memory_space=pltpu.HBM)


def call(kernel, out_shape, in_specs, args, *, flops, size, scratch=(), limit=16 << 20):
    return pl.pallas_call(
        kernel,
        out_shape=out_shape,
        in_specs=in_specs,
        out_specs=jax.tree.map(lambda _: VMEM, out_shape),
        scratch_shapes=list(scratch),
        compiler_params=pltpu.CompilerParams(vmem_limit_bytes=limit),
        cost_estimate=pl.CostEstimate(flops=flops, bytes_accessed=size, transcendentals=0),
    )(*args)


def shape(*dims, dtype=BF16):
    return jax.ShapeDtypeStruct(dims, dtype)


def in_hbm(value):
    return pltpu.with_memory_space_constraint(value, pltpu.HBM)


def in_vmem(value):
    return pltpu.with_memory_space_constraint(value, pltpu.VMEM)


def shift(value, axis, size, by):
    return lax.ppermute(value, axis, [(i, (i + by) % size) for i in range(size)])


def three_parts(value):
    high = value.astype(BF16).astype(F32)
    middle = (value - high).astype(BF16).astype(F32)
    return high, middle, value - high - middle


def by_row(rows):
    sub = lax.broadcasted_iota(jnp.int32, (8, SLOT), 0)
    tile = jnp.zeros((8, SLOT), F32)
    for n, value in enumerate(rows):
        tile = jnp.where(sub == n, value, tile)
    return tile


def send_kernel(*refs):
    sources, hidden, outs = refs[:6], refs[6], refs[7:-9]
    *held, order, small, sems = refs[-9:]
    row = lax.axis_index("row").astype(jnp.int32)
    loads = [pltpu.make_async_copy(a, b, small.at[i]) for i, (a, b) in enumerate(zip(sources, held))]
    for load in loads:
        load.start()
    for load in loads:
        load.wait()
    dest_of, length_of, offset_of, group_of, reward_of, old_logp = held
    for slot in range(ROWS):
        order[lax.rem(lax.shift_right_logical(dest_of[slot], 2) - row + ROWS, ROWS)] = slot
    copies = []
    for c in range(len(CHUNKS)):
        for k in range(ROWS):
            copies.append(
                pltpu.make_async_copy(
                    hidden.at[
                        pl.ds(pl.multiple_of(order[k] * SLOT, SLOT), SLOT),
                        pl.ds(STARTS[c], CHUNKS[c]),
                    ],
                    outs[c * ROWS + k].at[pl.ds(0, SLOT), :],
                    sems.at[c * ROWS + k],
                )
            )
            copies[-1].start()
    lane = lax.broadcasted_iota(jnp.int32, (1, SLOT), 1)
    shared = []
    for entries in (reward_of, group_of, length_of):
        value = jnp.zeros((1, SLOT), F32)
        for i in range(ROWS):
            value = jnp.where(lane == i, entries[i].astype(F32), value)
        shared.append(value)
    for k in range(ROWS):
        slot = order[k]
        place = offset_of[slot]
        high = lax.shift_right_logical(place, 4)
        low = place - high * 16
        own = by_row(
            (
                length_of[slot].astype(F32),
                high.astype(F32),
                low.astype(F32),
                *three_parts(old_logp[pl.ds(slot, 1), :]),
            )
        )
        common = by_row((*three_parts(shared[0]), shared[1], shared[2], slot.astype(F32)))
        outs[k][SLOT : SLOT + 8, 0:SLOT] = own.astype(BF16)
        outs[k][SLOT : SLOT + 8, SLOT : 2 * SLOT] = common.astype(BF16)
        if CHUNKS[0] > 2 * SLOT:
            outs[k][SLOT : SLOT + 8, 2 * SLOT :] = jnp.zeros((8, CHUNKS[0] - 2 * SLOT), BF16)
    for copy in copies:
        copy.wait()


def send_blocks(*args):
    outs = [shape(SLOT + (8 if c == 0 else 0), CHUNKS[c]) for c in range(len(CHUNKS)) for _ in range(ROWS)]
    flat = call(
        send_kernel,
        outs,
        [HBM] * 7,
        [in_hbm(a) for a in args],
        flops=1000000,
        size=4 << 20,
        scratch=[
            *[pltpu.SMEM((ROWS,), jnp.int32)] * 4,
            pltpu.SMEM((ROWS,), F32),
            pltpu.VMEM((ROWS, SLOT), F32),
            pltpu.SMEM((ROWS,), jnp.int32),
            pltpu.SemaphoreType.DMA((6,)),
            pltpu.SemaphoreType.DMA((len(outs),)),
        ],
    )
    return [flat[c * ROWS : (c + 1) * ROWS] for c in range(len(CHUNKS))]


def fetch_kernel(*refs):
    count = (len(refs) - 1) // 2
    copies = [pltpu.make_async_copy(refs[i], refs[count + i], refs[-1].at[i]) for i in range(count)]
    for copy in copies:
        copy.start()
    for copy in copies:
        copy.wait()


def fetch(*values):
    return call(
        fetch_kernel,
        [pltpu.VMEM(v.shape, v.dtype) for v in values],
        [HBM] * len(values),
        [in_hbm(v) for v in values],
        flops=1000,
        size=8 << 20,
        scratch=[pltpu.SemaphoreType.DMA((len(values),))],
    )


def pack_kernel(first, *refs):
    blocks = refs[:ROWS]
    if first:
        upper, lower, positions, notes = refs[ROWS:]
    else:
        notes, upper, lower = refs[ROWS:]
    place = lax.broadcasted_iota(jnp.int32, (PACK, SLOT), 0).astype(F32)
    lane = lax.broadcasted_iota(jnp.int32, (PACK, SLOT), 1).astype(F32)
    picks = []
    within = jnp.zeros((PACK, SLOT), F32)
    for k in range(ROWS):
        if first:
            notes[8 * k : 8 * k + 8, :] = blocks[k][SLOT : SLOT + 8, 0 : 2 * SLOT]
            note = blocks[k][SLOT : SLOT + 8, 0:SLOT].astype(F32)
        else:
            note = notes[8 * k : 8 * k + 8, 0:SLOT].astype(F32)
        length = note[0:1, :]
        offset = note[1:2, :] * 16.0 + note[2:3, :]
        hit = (place - offset == lane) & (lane < length)
        picks.append(jnp.where(hit, 1.0, 0.0).astype(BF16))
        if first:
            within = within + jnp.where(hit, lane, 0.0)
    pick = jnp.concatenate(picks, 1)
    rows = jnp.concatenate([b[0:SLOT, :] for b in blocks], 0)
    packed = jnp.dot(pick, rows, preferred_element_type=F32).astype(BF16)
    upper[...] = packed[: PACK // 2]
    lower[...] = packed[PACK // 2 :]
    if first:
        positions[...] = jnp.broadcast_to(jnp.sum(within, 1, keepdims=True), (PACK, SLOT))


def pack(c, blocks, notes=None):
    outs = [shape(PACK // 2, CHUNKS[c]), shape(PACK // 2, CHUNKS[c])]
    args = list(blocks)
    if notes is None:
        outs += [shape(PACK, SLOT, dtype=F32), shape(8 * ROWS, 2 * SLOT)]
    else:
        args.append(notes)
    return call(
        functools.partial(pack_kernel, notes is None),
        outs,
        [VMEM] * len(args),
        args,
        flops=2 * PACK * 8 * SLOT * CHUNKS[c],
        size=2 << 20,
    )


def gather_halves(upper, lower):
    left_upper = shift(upper, "mp", SHARDS, 1)
    right_lower = shift(lower, "mp", SHARDS, -1)
    left_lower = shift(lower, "mp", SHARDS, 1)
    right_upper = shift(upper, "mp", SHARDS, -1)
    far_upper = shift(left_upper, "mp", SHARDS, 1)
    far_lower = shift(right_lower, "mp", SHARDS, -1)
    return {
        0: (upper, lower),
        3: (left_upper, left_lower),
        1: (right_upper, right_lower),
        2: (far_upper, far_lower),
    }


def project_kernel(c, steps, carried, last, *refs):
    width = CHUNKS[c]
    refs = list(refs)
    halves = [(refs.pop(0), refs.pop(0)) for _ in steps]
    gain, w_query, w_key, w_value = [refs.pop(0) for _ in range(4)]
    if carried:
        total_in, square_in = refs.pop(0), refs.pop(0)
    if last:
        bias, cosine, sine = refs.pop(0), refs.pop(0), refs.pop(0)
        queries, keys, values = refs.pop(0), refs.pop(0), refs.pop(0)
    else:
        total_out, square_out = refs.pop(0), refs.pop(0)
    own = refs
    me = lax.axis_index("mp").astype(jnp.int32)
    begin = pl.multiple_of(lax.rem(me, 2) * SLOT, SLOT)
    for i, (upper, lower) in enumerate(halves):
        own[i][...] = jnp.where(
            me < 2, upper[pl.ds(begin, SLOT), :], lower[pl.ds(begin, SLOT), :]
        )
    half = PACK // 2
    sources = [lax.rem(me + step, SHARDS) for step in steps]
    features = gain.shape[1]
    picked = [
        pl.ds(pl.multiple_of(source * features + STARTS[c], SLOT), width) for source in sources
    ]

    def weights(i, tile):
        if tile < 3:
            return w_query[picked[i], tile * 256 : tile * 256 + 256]
        if tile == 3:
            return jnp.concatenate([w_query[picked[i], 768:896], w_key[picked[i], :]], 1)
        return w_value[picked[i], :]

    for h in range(2):
        rows = slice(h * half, (h + 1) * half)
        square = jnp.zeros((half, SLOT), F32)
        scaled = []
        for i, pair in enumerate(halves):
            wide = pair[h][...].astype(F32)
            for j in range(0, width, SLOT):
                square = square + wide[:, j : j + SLOT] * wide[:, j : j + SLOT]
            factor = gain[pl.ds(sources[i], 1), STARTS[c] : STARTS[c] + width]
            scaled.append((wide * factor).astype(BF16))
        if carried:
            square = square + square_in[rows, :]
        if last:
            mean = jnp.sum(square, 1, keepdims=True) * (1.0 / (SHARDS * features))
            inverse = lax.rsqrt(mean + norm_eps)
        else:
            square_out[rows, :] = square
        for tile in range(5):
            columns = slice(tile * 256, min(tile * 256 + 256, 9 * HEAD))
            part = None
            for i in range(len(steps)):
                term = jnp.dot(scaled[i], weights(i, tile), preferred_element_type=F32)
                part = term if part is None else part + term
            if carried:
                part = part + total_in[rows, columns]
            if not last:
                total_out[rows, columns] = part
                continue
            part = part * inverse + bias[0:1, columns]
            for n in range(part.shape[1] // HEAD):
                head = part[:, n * HEAD : (n + 1) * HEAD]
                at = 2 * tile + n
                if at < 8:
                    head = head * cosine[rows, :] + pltpu.roll(head, HEAD // 2, 1) * sine[rows, :]
                if at < 7:
                    queries[rows, at * HEAD : (at + 1) * HEAD] = head.astype(BF16)
                elif at == 7:
                    keys[rows, :] = head.astype(BF16)
                else:
                    values[rows, :] = head.astype(BF16)


def project(c, steps, pieces, weights, carried=None, tables=None):
    width = CHUNKS[c]
    columns = 9 * HEAD
    args = []
    for step in steps:
        args += list(pieces[step])
    args += list(weights)
    if carried is not None:
        args += list(carried)
    if tables is None:
        outs = [shape(PACK, columns, dtype=F32), shape(PACK, SLOT, dtype=F32)]
    else:
        args += list(tables)
        outs = [shape(PACK, 7 * HEAD), shape(PACK, HEAD), shape(PACK, HEAD)]
    keep = len(outs)
    outs += [shape(SLOT, width)] * len(steps)
    result = call(
        functools.partial(project_kernel, c, steps, carried is not None, tables is not None),
        outs,
        [VMEM] * len(args),
        args,
        flops=2 * PACK * width * len(steps) * columns,
        size=len(steps) * width * (columns + PACK) * 2 + (4 << 20),
    )
    return result[:keep], dict(zip(steps, result[keep:]))


def attend_kernel(steps, queries, keys, values, positions, w_out, *outs):
    me = lax.axis_index("mp").astype(jnp.int32)
    heads = queries.shape[1] // HEAD
    for n, step in enumerate(steps):
        block = lax.rem(me + step, SHARDS)
        begin = pl.multiple_of(block * SLOT, SLOT)
        window = pl.multiple_of(jnp.maximum(block - 1, 0) * SLOT, SLOT)
        row = begin.astype(F32) + lax.broadcasted_iota(jnp.int32, (SLOT, SLOT), 0).astype(F32)
        lane = window.astype(F32) + lax.broadcasted_iota(jnp.int32, (SLOT, SLOT), 1).astype(F32)
        row_start = row - positions[pl.ds(begin, SLOT), :]
        allowed = jnp.concatenate(
            [(lane >= row_start) & (lane <= row), (lane + SLOT >= row_start) & (lane + SLOT <= row)], 1
        )
        all_keys = keys[pl.ds(window, 2 * SLOT), :]
        all_values = values[pl.ds(window, 2 * SLOT), :]
        mixed = []
        for h in range(heads):
            scores = lax.dot_general(
                queries[pl.ds(begin, SLOT), h * HEAD : (h + 1) * HEAD],
                all_keys,
                (((1,), (1,)), ((), ())),
                preferred_element_type=F32,
            )
            scores = jnp.where(allowed, scores * HEAD ** (-0.5), mask_fill)
            exponent = jnp.exp(scores - jnp.max(scores, 1, keepdims=True))
            weights = (exponent / jnp.sum(exponent, 1, keepdims=True)).astype(BF16)
            mixed.append(
                jnp.dot(weights, all_values, preferred_element_type=F32).astype(BF16)
            )
        mixed = jnp.concatenate(mixed, 1)
        for j in range(0, w_out.shape[1], 512):
            part = jnp.dot(mixed, w_out[:, j : j + 512], preferred_element_type=F32).astype(BF16)
            outs[2 * n][:, j : j + 512] = part[: SLOT // 2]
            outs[2 * n + 1][:, j : j + 512] = part[SLOT // 2 :]


def attend(steps, queries, keys, values, positions, w_out):
    width = w_out.shape[1]
    return call(
        functools.partial(attend_kernel, steps),
        [shape(SLOT // 2, width)] * (2 * len(steps)),
        [VMEM] * 5,
        (queries, keys, values, positions, w_out),
        flops=len(steps) * 2 * SLOT * w_out.shape[0] * (width + 4 * SLOT),
        size=8 << 20,
    )


def add_kernel(a, b, c, d, ab, cd):
    ab[...] = (a[...].astype(F32) + b[...].astype(F32)).astype(BF16)
    cd[...] = (c[...].astype(F32) + d[...].astype(F32)).astype(BF16)


def sort_kernel(notes, stats_out, mine_out):
    lane = lax.broadcasted_iota(jnp.int32, (1, SLOT), 1)
    for k in range(ROWS):
        own = notes[8 * k : 8 * k + 8, 0:SLOT].astype(F32)
        common = notes[8 * k : 8 * k + 8, SLOT : 2 * SLOT].astype(F32)
        rewards = common[0:1, :] + common[1:2, :] + common[2:3, :]
        groups = common[3:4, :]
        picked = lane.astype(F32) == common[5:6, :]
        stats_out[k : k + 1, :] = (
            rewards + pltpu.roll(groups, 8, 1) + pltpu.roll(common[4:5, :], 16, 1)
        )
        info = jnp.where(lane == 26, own[1:2, :] * 16.0 + own[2:3, :], 0.0)
        info = jnp.where(lane == 27, own[0:1, :], info)
        for n, value in ((24, rewards), (25, groups)):
            info = jnp.where(
                lane == n, jnp.sum(jnp.where(picked, value, 0.0), 1, keepdims=True), info
            )
        mine_out[k : k + 1, 0:SLOT] = own[3:4, :] + own[4:5, :] + own[5:6, :]
        mine_out[k : k + 1, SLOT:] = info


def note_kernel(stats_a, stats_b, stats_c, stats_d, mine_ref, log_normalizer, base_out, adv_out, occupied_out, scale_out):
    me = lax.axis_index("mp").astype(jnp.int32)
    lane32 = lax.broadcasted_iota(jnp.int32, (COLS * ROWS, SLOT), 1)
    rewards = jnp.concatenate([stats_a[...], stats_b[...], stats_c[...], stats_d[...]], 0)
    groups = pltpu.roll(rewards, SLOT - 8, 1)
    lengths = pltpu.roll(rewards, SLOT - 16, 1)
    valid = lane32 < 8
    place = (lax.broadcasted_iota(jnp.int32, (SLOT, SLOT), 0) + me * SLOT).astype(F32)
    lane_int = lax.broadcasted_iota(jnp.int32, (SLOT, SLOT), 1)
    lane = lane_int.astype(F32)
    one_lane = lax.broadcasted_iota(jnp.int32, (1, SLOT), 1)

    def total(value):
        return jnp.sum(jnp.sum(value, 1, keepdims=True), 0, keepdims=True)

    old = jnp.zeros((SLOT, SLOT), F32)
    adv = jnp.zeros((SLOT, SLOT), F32)
    occupied = jnp.zeros((SLOT, SLOT), F32)
    for r in range(ROWS):
        mine = mine_ref[r : r + 1, :]
        info = mine[:, SLOT:]

        def entry(at):
            return jnp.sum(jnp.where(one_lane == at, info, 0.0), 1, keepdims=True)

        reward, group, offset, length = entry(24), entry(25), entry(26), entry(27)
        member = valid & (groups == group)
        mean = total(jnp.where(member, rewards, 0.0)) / GROUP_SIZE
        centered = jnp.where(member, rewards - mean, 0.0)
        spread = total(centered * centered) / GROUP_SIZE
        advantage = (reward - mean) / jnp.maximum(jnp.sqrt(spread), std_floor)
        hit = (place - offset == lane) & (lane < length)
        old = old + jnp.where(hit, mine[:, :SLOT], 0.0)
        adv = adv + jnp.where(hit, advantage, 0.0)
        occupied = occupied + jnp.where(hit, 1.0, 0.0)
    diagonal = lane_int == lax.broadcasted_iota(jnp.int32, (SLOT, SLOT), 0)
    old = old + jnp.where(diagonal, log_normalizer[...], 0.0)
    base_out[...] = jnp.sum(old, 1, keepdims=True)
    adv_out[...] = jnp.sum(adv, 1, keepdims=True)
    occupied_out[...] = jnp.sum(occupied, 1, keepdims=True)
    scale_out[...] = -1.0 / total(jnp.where(valid, lengths, 0.0))


def prepare_kernel(keys, *refs):
    refs = list(refs)
    own = [refs.pop(0) for _ in keys]
    own_a, raw_a, own_b, raw_b, gain, chosen, known, factor = refs
    me = lax.axis_index("mp").astype(jnp.int32)
    for (c, step), resid in zip(keys, own):
        start = lax.rem(me + step, SHARDS) * sum(CHUNKS) + STARTS[c]
        for j in range(0, CHUNKS[c], SLOT):
            at = pl.ds(pl.multiple_of(start + j, SLOT), SLOT)
            branch = jnp.concatenate(
                [
                    own_a[:, at].astype(F32) + raw_a[:, at].astype(F32),
                    own_b[:, at].astype(F32) + raw_b[:, at].astype(F32),
                ],
                0,
            )
            known[:, at] = resid[:, j : j + SLOT].astype(F32) + branch
    factor[...] = gain[...].astype(F32) * chosen[...].astype(F32)


def finish_kernel(known, factor, two_a, two_b, base, adv, occupied, objective_out, total_out):
    width = known.shape[1]
    square = jnp.zeros((SLOT, SLOT), F32)
    product = jnp.zeros((SLOT, SLOT), F32)
    for j in range(0, width, SLOT):
        at = slice(j, j + SLOT)
        two = jnp.concatenate([two_a[:, at].astype(F32), two_b[:, at].astype(F32)], 0)
        rows = (known[:, at] + two).astype(BF16).astype(F32)
        square = square + rows * rows
        product = product + rows * factor[:, at]
    mean = jnp.sum(square, 1, keepdims=True) * (1.0 / width)
    logits = jnp.sum(product, 1, keepdims=True) * lax.rsqrt(mean + norm_eps)
    ratios = jnp.exp(logits - base[...])
    bounded = jnp.clip(ratios, 1.0 - clip_low, 1.0 + clip_high)
    value = jnp.minimum(ratios * adv[...], bounded * adv[...])
    value = jnp.where(occupied[...] > 0.5, value, 0.0)
    diagonal = lax.broadcasted_iota(jnp.int32, (SLOT, SLOT), 1) == lax.broadcasted_iota(
        jnp.int32, (SLOT, SLOT), 0
    )
    line = jnp.sum(jnp.where(diagonal, value, 0.0), 0, keepdims=True)
    objective_out[...] = line
    total = jnp.sum(line, 1, keepdims=True)
    total_out[...] = jnp.broadcast_to(total[None], (SLOT, 1, SLOT))


def body(
    hidden,
    old_logp,
    rewards,
    resp_dest,
    resp_len,
    resp_offset,
    prompt_group,
    attn_gain,
    w_query,
    q_bias,
    w_key,
    k_bias,
    w_value,
    v_bias,
    w_out,
    final_gain,
    chosen_rows,
    log_normalizer,
):
    sent = send_blocks(
        resp_dest,
        resp_len,
        resp_offset,
        prompt_group,
        rewards,
        old_logp.reshape(ROWS, SLOT),
        hidden,
    )
    received = [
        [blocks[0]] + [shift(blocks[k], "row", ROWS, k) for k in range(1, ROWS)] for blocks in sent
    ]
    upper, lower, positions, notes = pack(0, received[0])
    first = gather_halves(upper, lower)
    second = gather_halves(*pack(1, received[1], notes))

    gain = attn_gain.astype(F32).reshape(SHARDS, -1)
    last_gain = final_gain[None, :]
    bias = jnp.concatenate([q_bias, k_bias, v_bias]).astype(F32)[None, :]
    exponents = (jnp.arange(HEAD, dtype=F32) % (HEAD // 2)) * (2.0 / HEAD)
    angles = positions * (rope_theta ** (-exponents))[None, :]
    sign = jnp.where(jnp.arange(HEAD) < HEAD // 2, -1.0, 1.0)
    cosine, sine = jnp.cos(angles), jnp.sin(angles) * sign[None, :]
    gain, last_gain, bias, cosine, sine, w_query, w_key, w_value, w_out = lax.optimization_barrier(
        (gain, last_gain, bias, cosine, sine, w_query, w_key, w_value, w_out)
    )
    tables = (bias, cosine, sine)
    weights = (gain, *[in_vmem(w) for w in fetch(w_query, w_key, w_value)])
    w_out = in_vmem(fetch(w_out)[0])
    stats, mine = call(
        sort_kernel,
        [shape(ROWS, SLOT, dtype=F32), shape(ROWS, 2 * SLOT, dtype=F32)],
        [VMEM],
        (notes,),
        flops=100000,
        size=1 << 17,
    )

    carried, own_first = project(0, (0, 1, 3, 2), first, weights)
    carried, own_near = project(1, (0, 1, 3), second, weights, carried)
    (queries, keys, values), own_far = project(1, (2,), second, weights, carried, tables)

    attend_to = functools.partial(
        attend,
        queries=queries,
        keys=keys,
        values=values,
        positions=positions,
        w_out=w_out,
    )
    far_a, far_b = attend_to((2,))
    from_left = shift(far_a, "mp", SHARDS, 1)
    from_right = shift(far_b, "mp", SHARDS, -1)
    right_a, right_b, left_a, left_b = attend_to((1, 3))
    raw_b = shift(right_b, "mp", SHARDS, 1)
    raw_a = shift(left_a, "mp", SHARDS, -1)
    own_a, own_b = attend_to((0,))
    stats, own_a = lax.optimization_barrier((stats, own_a))
    base, adv, occupied, scale = call(
        note_kernel,
        [shape(SLOT, 1, dtype=F32)] * 3 + [shape(1, 1, dtype=F32)],
        [VMEM] * 6,
        (
            stats,
            *[shift(stats, "col", COLS, k) for k in range(1, COLS)],
            mine,
            log_normalizer[None, :],
        ),
        flops=4000000,
        size=1 << 18,
    )
    sum_a, sum_b = call(
        add_kernel,
        [shape(*far_a.shape)] * 2,
        [VMEM] * 4,
        (right_a, from_left, left_b, from_right),
        flops=1000000,
        size=3 << 20,
    )
    two_a = shift(sum_a, "mp", SHARDS, 1)
    two_b = shift(sum_b, "mp", SHARDS, -1)

    own = {(0, s): v for s, v in own_first.items()}
    own |= {(1, s): v for s, v in (own_near | own_far).items()}
    names = sorted(own)
    known, factor = call(
        functools.partial(prepare_kernel, names),
        [shape(SLOT, w_out.shape[1], dtype=F32)] * 2,
        [VMEM] * (len(names) + 6),
        (*[own[n] for n in names], own_a, raw_a, own_b, raw_b, last_gain, chosen_rows),
        flops=4000000,
        size=6 << 20,
    )
    objective, totals = call(
        finish_kernel,
        [shape(1, SLOT, dtype=F32), shape(SLOT, 1, SLOT, dtype=F32)],
        [VMEM] * 7,
        (known, factor, two_a, two_b, base, adv, occupied),
        flops=8000000,
        size=6 << 20,
    )
    sums = lax.all_to_all(totals, ROW_COL_MP, 0, 0, tiled=True)
    loss = jnp.sum(sums[:, 0, 0]) * scale[0, 0]
    return objective.reshape(SLOT), loss


def solution(mesh):
    placed = (
        P(ROW_COL, "mp"),
        P(ROW_COL),
        P(ROW_COL),
        P(ROW_COL),
        P(ROW_COL),
        P(ROW_COL),
        P(ROW_COL),
        P(),
        P(None, "mp"),
        P("mp"),
        P(None, "mp"),
        P("mp"),
        P(None, "mp"),
        P("mp"),
        P("mp", None),
        P(),
        P(ROW_COL_MP, None),
        P(ROW_COL_MP),
    )

    return jax.shard_map(
        body, mesh=mesh, in_specs=placed, out_specs=(P(ROW_COL_MP), P()), check_vma=False
    )
```

time: 240 us -> 129 us (0.54)
  waiting for transfers between devices: 94.2 us -> 28.3 us
  matrix products: 35.1 us -> 0 us
  starting transfers between devices: 18.4 us -> 50.7 us
  Pallas kernels: 0 us -> 27.3 us
  local copies, waits for them, and re-layouts: 21.2 us -> 0.74 us
  blocking collectives: 34.8 us -> 16.1 us
  other arithmetic: 19.2 us -> 1.72 us
  between operations: 16.8 us -> 3.33 us
    ppermute x0 -> x35, starting transfers between devices: none -> 50.7 us  [shift(): lax.ppermute(value, axis, [(i, (i + by) % size) for i in range(size)])]
    all_gather x1 -> x0, waiting for transfers between devices: 41.8 us -> none  [body(): gathered = lax.all_gather(packed, 'mp', axis=1, tiled=True)]
    dot_general x15 -> x0, matrix products: 35.1 us -> none  [the longest x1 8.28 us: body(): jnp.dot(pieces, w_out, preferred_element_type=jnp.float32)]
    psum x4 -> x0, blocking collectives: 34.8 us -> none  [over_axes(): value = lax.psum(value, axis)]
    all_to_all x4 -> x0, waiting for transfers between devices: 34.8 us -> none  [the longest x1 22.9 us: body(): lax.all_to_all(send_rows, ROW, split_axis=0, concat_axis=0, tiled=True)]
    ppermute x0 -> x35, waiting for transfers between devices: none -> 28.3 us  [shift(): lax.ppermute(value, axis, [(i, (i + by) % size) for i in range(size)])]
    pallas_call x0 -> x16, Pallas kernels: none -> 27.3 us  [call(): pl.pallas_call(kernel, out_shape=out_shape, in_specs=in_specs, out_specs=...]
    all_to_all x4 -> x0, starting transfers between devices: 18.3 us -> none  [the longest x1 5.42 us: sent_to_all(): return lax.all_to_all(copies, axis, split_axis=0, concat_axis=0, tiled=True)]
  transfers between devices with their start and end apart: 6 -> 35, of which waited for: 6 -> 14; matrix products, arithmetic and copies ran while one was open for 5% -> 1% of each run, Pallas kernels for 0% -> 16%
where the time goes in v1:
time: 129 us; the launch traced here: 128 us
  starting transfers between devices  50.7 us (39%)
  waiting for transfers between devices  28.3 us (22%)
  Pallas kernels  27.3 us (21%)
  blocking collectives  16.1 us (12%)
  between operations  3.33 us (3%)
  other arithmetic  1.72 us (1%)
    ppermute x35, starting transfers between devices, shift(): lax.ppermute(value, axis, [(i, (i + by) % size) for i in range(size)])  50.7 us
    ppermute x35, waiting for transfers between devices, shift(): lax.ppermute(value, axis, [(i, (i + by) % size) for i in range(size)])  28.3 us
    pallas_call x16, Pallas kernels, call(): pl.pallas_call(kernel, out_shape=out_shape, in_specs=in_specs, out_specs=...  27.3 us
    all_to_all x1, blocking collectives, body(): sums = lax.all_to_all(totals, ROW_COL_MP, 0, 0, tiled=True)  16.1 us
  transfers between devices with their start and end apart: 35, of which 14 were waited for; matrix products, arithmetic and copies ran while one was open for 1% of the time, Pallas kernels for 16%

profile of v1, /device:TPU:0, one launch (start us, length us, event | category | flops | bytes accessed | tf_op | source)
XLA Modules:
  0.0 128.3 jit_solution(10035133434476515584)
XLA Ops:
  0.7 2.6 %shard_map.185 = (bf16[136,384]{1,0:T(8,128)(2,1)S(1)}, bf16[136,384]{1,0:T(8,128)(2,1)S(1)}, bf16[136,384]{1,0:T(8,128)(2,1)S(1)}, bf16[136,384]{1,0:T(8,128)(2...) custom-call(s32[8]{0:T(128)} %refs_0_.1, ...), custom_call_target="tpu_custom_call" | custom-call | flops 1000000 | bytes 4194304 | tf_op jit(solution)/shard_map/pallas_call | solution.py:38
  5.1 2.2 %collective-permute-start.2 = (bf16[136,384]{1,0:T(8,128)(2,1)S(1)}, bf16[136,384]{1,0:T(8,128)(2,1)S(1)}, u32[]{:S(2)}, u32[]{:S(2)}) collective-permute-start(bf16[136,384]{1,0:T(8,128)(2,1)S(1)} %get-tuple-element.76), channel_id=1, source_target_pairs={{0,48},{16,64},{32,80},{48,96},{64,112},{80,0},{96,16},{112,32},{1... | collective-permute-start | bytes 313352 | tf_op jit(solution)/shard_map/ppermute | solution.py:62
  10.4 2.9 %collective-permute-start.4 = (bf16[136,384]{1,0:T(8,128)(2,1)S(1)}, bf16[136,384]{1,0:T(8,128)(2,1)S(1)}, u32[]{:S(2)}, u32[]{:S(2)}) collective-permute-start(bf16[136,384]{1,0:T(8,128)(2,1)S(1)} %get-tuple-element.78), channel_id=1, source_target_pairs={{0,80},{16,96},{32,112},{48,0},{64,16},{80,32},{96,48},{112,64},{1... | collective-permute-start | bytes 313352 | tf_op jit(solution)/shard_map/ppermute | solution.py:62
  21.2 2.8 %collective-permute-start.17 = (bf16[128,512]{1,0:T(8,128)(2,1)S(1)}, bf16[128,512]{1,0:T(8,128)(2,1)S(1)}, u32[]{:S(2)}, u32[]{:S(2)}) collective-permute-start(bf16[128,512]{1,0:T(8,128)(2,1)S(1)} %get-tuple-element.100), channel_id=1, source_target_pairs={{0,80},{16,96},{32,112},{48,0},{64,16},{80,32},{96,48},{112,64},{1... | collective-permute-start | bytes 393224 | tf_op jit(solution)/shard_map/ppermute | solution.py:62
  24.3 2.6 %collective-permute-start.19 = (bf16[128,512]{1,0:T(8,128)(2,1)S(1)}, bf16[128,512]{1,0:T(8,128)(2,1)S(1)}, u32[]{:S(2)}, u32[]{:S(2)}) collective-permute-start(bf16[128,512]{1,0:T(8,128)(2,1)S(1)} %get-tuple-element.102), channel_id=1, source_target_pairs={{0,112},{16,0},{32,16},{48,32},{64,48},{80,64},{96,80},{112,96},{1... | collective-permute-start | bytes 393224 | tf_op jit(solution)/shard_map/ppermute | solution.py:62
  28.5 2.8 %collective-permute-start.7 = (bf16[256,384]{1,0:T(8,128)(2,1)S(1)}, bf16[256,384]{1,0:T(8,128)(2,1)S(1)}, u32[]{:S(2)}, u32[]{:S(2)}) collective-permute-start(bf16[256,384]{1,0:T(8,128)(2,1)S(1)} %get-tuple-element.81.refs_0_), channel_id=1, source_target_pairs={{0,3},{1,0},{2,1},{3,2},{4,7},{5,4},{6,5},{7,6},{8,11},{9,8},{10,9... | collective-permute-start | bytes 589832 | tf_op jit(solution)/shard_map/ppermute | solution.py:62
  31.4 3.2 %collective-permute-start.8 = (bf16[256,384]{1,0:T(8,128)(2,1)S(1)}, bf16[256,384]{1,0:T(8,128)(2,1)S(1)}, u32[]{:S(2)}, u32[]{:S(2)}) collective-permute-start(bf16[256,384]{1,0:T(8,128)(2,1)S(1)} %get-tuple-element.82.refs_1_), channel_id=1, source_target_pairs={{0,3},{1,0},{2,1},{3,2},{4,7},{5,4},{6,5},{7,6},{8,11},{9,8},{10,9... | collective-permute-start | bytes 589832 | tf_op jit(solution)/shard_map/ppermute | solution.py:62
  35.3 3.3 %collective-permute-start.21 = (bf16[256,512]{1,0:T(8,128)(2,1)S(1)}, bf16[256,512]{1,0:T(8,128)(2,1)S(1)}, u32[]{:S(2)}, u32[]{:S(2)}) collective-permute-start(bf16[256,512]{1,0:T(8,128)(2,1)S(1)} %get-tuple-element.105.refs_1_), channel_id=1, source_target_pairs={{0,3},{1,0},{2,1},{3,2},{4,7},{5,4},{6,5},{7,6},{8,11},{9,8},{10,9... | collective-permute-start | bytes 786440 | tf_op jit(solution)/shard_map/ppermute | solution.py:62
  39.9 3.7 %collective-permute-start.20 = (bf16[256,512]{1,0:T(8,128)(2,1)S(1)}, bf16[256,512]{1,0:T(8,128)(2,1)S(1)}, u32[]{:S(2)}, u32[]{:S(2)}) collective-permute-start(bf16[256,512]{1,0:T(8,128)(2,1)S(1)} %get-tuple-element.104.refs_0_), channel_id=1, source_target_pairs={{0,3},{1,0},{2,1},{3,2},{4,7},{5,4},{6,5},{7,6},{8,11},{9,8},{10,9... | collective-permute-start | bytes 786440 | tf_op jit(solution)/shard_map/ppermute | solution.py:62
  45.5 3.7 %collective-permute-start.12 = (bf16[256,384]{1,0:T(8,128)(2,1)S(1)}, bf16[256,384]{1,0:T(8,128)(2,1)S(1)}, u32[]{:S(2)}, u32[]{:S(2)}) collective-permute-start(bf16[256,384]{1,0:T(8,128)(2,1)S(1)} %collective-permute-done.8.refs_3_), channel_id=1, source_target_pairs={{0,3},{1,0},{2,1},{3,2},{4,7},{5,4},{6,5},{7,6},{8,11},{9,8},{10,9... | collective-permute-start | bytes 589832 | tf_op jit(solution)/shard_map/ppermute | solution.py:62
  50.1 2.8 %shard_map.193.w_out = bf16[896,3584]{1,0:T(8,128)(2,1)S(1)} custom-call(bf16[896,3584]{1,0:T(8,128)(2,1)} %refs_0_.3), custom_call_target="tpu_custom_call" | custom-call | flops 1000 | bytes 8388608 | tf_op jit(solution)/shard_map/pallas_call | solution.py:38
  53.0 3.3 %shard_map.187 = (bf16[3584,896]{1,0:T(8,128)(2,1)S(1)}, bf16[3584,128]{1,0:T(8,128)(2,1)S(1)}, bf16[3584,128]{1,0:T(8,128)(2,1)S(1)}) custom-call(bf16[3584,896]{1,0:T(8,128)(2,1)} %refs_0_.2, bf16[3584,128]{1,0:T(8,128)(2,1)} %refs_1_.2, bf16[3584,128]{1,0:T(8,128)(2,1)} %refs_2_.2), custom_call_target="tpu_custom_call" | custom-call | flops 1000 | bytes 8388608 | tf_op jit(solution)/shard_map/pallas_call | solution.py:38
  56.4 2.6 %collective-permute-done.11.refs_6_ = bf16[256,384]{1,0:T(8,128)(2,1)S(1)} collective-permute-done((bf16[256,384]{1,0:T(8,128)(2,1)S(1)}, bf16[256,384]{1,0:T(8,128)(2,1)S(1)}, u32[]{:S(2)}, u32[]{:S(2)}) %collective-permute-start.11) | collective-permute-done | bytes 196640 | tf_op jit(solution)/shard_map/ppermute | solution.py:62
  59.6 2.8 %shard_map.188 = (f32[512,1152]{1,0:T(8,128)S(1)}, f32[512,128]{1,0:T(8,128)S(1)}, bf16[128,384]{1,0:T(8,128)(2,1)S(1)}, bf16[128,384]{1,0:T(8,128)(2,1)S(1)}, b...) custom-call(bf16[256,384]{1,0:T(8,128)(2,1)S(1)} %get-tuple-element.81.refs_0_, ...), custom_call_target="tpu_custom_call" | custom-call | flops 1811939328 | bytes 9306112 | tf_op jit(solution)/shard_map/pallas_call | solution.py:38
  62.4 2.3 %shard_map.190 = (f32[512,1152]{1,0:T(8,128)S(1)}, f32[512,128]{1,0:T(8,128)S(1)}, bf16[128,512]{1,0:T(8,128)(2,1)S(1)}, bf16[128,512]{1,0:T(8,128)(2,1)S(1)}, bf16[128,512]{1,0:T(8,128)(2,1)S(1)}) custom-call(bf16[256,512]{1,0:T(8,128)(2,1)S(1)} %get-tuple-element.104.refs_0_, bf16[256,512]{1,0:T(8,128)(2,1)S(1)} %get-tuple-element.105.refs_1_, ...), custom_call_target="tpu_custom_call" | custom-call | flops 1811939328 | bytes 9306112 | tf_op jit(solution)/shard_map/pallas_call | solution.py:38
  66.0 2.1 %collective-permute-done.25.refs_1_ = bf16[256,512]{1,0:T(8,128)(2,1)S(1)} collective-permute-done((bf16[256,512]{1,0:T(8,128)(2,1)S(1)}, bf16[256,512]{1,0:T(8,128)(2,1)S(1)}, u32[]{:S(2)}, u32[]{:S(2)}) %collective-permute-start.25) | collective-permute-done | bytes 262176 | tf_op jit(solution)/shard_map/ppermute | solution.py:62
  69.1 2.1 %shard_map.197 = (bf16[64,3584]{1,0:T(8,128)(2,1)S(1)}, bf16[64,3584]{1,0:T(8,128)(2,1)S(1)}) custom-call(bf16[512,896]{1,0:T(8,128)(2,1)S(1)} %get-tuple-element.118.queries, bf16[512,128]{1,0:T(8,128)(2,1)S(1)} %get-tuple-element.119.keys, bf16[512,128]{1,0:T(8,128)(2,1)S(1)} %get-tuple-element.120.values, f32[512,128]{1,0:T(8,128)S(1)} %get-tuple-element.83.positions, ...), custom_call_target="tpu_custom_call" | custom-call | flops 939524096 | bytes 8388608 | tf_op jit(solution)/shard_map/pallas_call | solution.py:38
  71.3 3.2 %collective-permute-start.29 = (bf16[64,3584]{1,0:T(8,128)(2,1)S(1)}, bf16[64,3584]{1,0:T(8,128)(2,1)S(1)}, u32[]{:S(2)}, u32[]{:S(2)}) collective-permute-start(bf16[64,3584]{1,0:T(8,128)(2,1)S(1)} %get-tuple-element.133), channel_id=1, source_target_pairs={{0,3},{1,0},{2,1},{3,2},{4,7},{5,4},{6,5},{7,6},{8,11},{9,8},{10,9... | collective-permute-start | bytes 1376264 | tf_op jit(solution)/shard_map/ppermute | solution.py:62
  74.5 3.7 %shard_map.195 = (bf16[64,3584]{1,0:T(8,128)(2,1)S(1)}, bf16[64,3584]{1,0:T(8,128)(2,1)S(1)}, bf16[64,3584]{1,0:T(8,128)(2,1)S(1)}, bf16[64,3584]{1,0:T(8,128)(2,1)S(1)}) custom-call(bf16[512,896]{1,0:T(8,128)(2,1)S(1)} %get-tuple-element.118.queries, bf16[512,128]{1,0:T(8,128)(2,1)S(1)} %get-tuple-element.119.keys, ...), custom_call_target="tpu_custom_call" | custom-call | flops 1879048192 | bytes 8388608 | tf_op jit(solution)/shard_map/pallas_call | solution.py:38
  80.3 5.6 %collective-permute-done.28.b = bf16[64,3584]{1,0:T(8,128)(2,1)S(1)} collective-permute-done((bf16[64,3584]{1,0:T(8,128)(2,1)S(1)}, bf16[64,3584]{1,0:T(8,128)(2,1)S(1)}, u32[]{:S(2)}, u32[]{:S(2)}) %collective-permute-start.28) | collective-permute-done | bytes 458784 | tf_op jit(solution)/shard_map/ppermute | solution.py:62
  86.4 3.3 %collective-permute-start.31 = (bf16[64,3584]{1,0:T(8,128)(2,1)S(1)}, bf16[64,3584]{1,0:T(8,128)(2,1)S(1)}, u32[]{:S(2)}, u32[]{:S(2)}) collective-permute-start(bf16[64,3584]{1,0:T(8,128)(2,1)S(1)} %get-tuple-element.135), channel_id=1, source_target_pairs={{0,3},{1,0},{2,1},{3,2},{4,7},{5,4},{6,5},{7,6},{8,11},{9,8},{10,9... | collective-permute-start | bytes 1376264 | tf_op jit(solution)/shard_map/ppermute | solution.py:62
  93.9 3.7 %collective-permute-done.32.stats_b = f32[8,128]{1,0:T(8,128)S(1)} collective-permute-done((f32[8,128]{1,0:T(8,128)S(1)}, f32[8,128]{1,0:T(8,128)S(1)}, u32[]{:S(2)}, u32[]{:S(2)}) %collective-permute-start.32) | collective-permute-done | bytes 4128 | tf_op jit(solution)/shard_map/ppermute | solution.py:62
  99.5 3.2 %collective-permute-done.33.stats_c = f32[8,128]{1,0:T(8,128)S(1)} collective-permute-done((f32[8,128]{1,0:T(8,128)S(1)}, f32[8,128]{1,0:T(8,128)S(1)}, u32[]{:S(2)}, u32[]{:S(2)}) %collective-permute-start.33) | collective-permute-done | bytes 4128 | tf_op jit(solution)/shard_map/ppermute | solution.py:62
  109.0 16.1 %all_to_all.5 = f32[128,1,128]{2,1,0:T(1,128)S(1)} all-to-all(f32[128,1,128]{2,1,0:T(1,128)S(1)} %get-tuple-element.142), channel_id=1, replica_groups=mesh['row'=8,'col'=4,'mp'=4] {'row','col','mp'}, dimensions={0} | all-to-all | bytes 131072 | tf_op jit(solution)/shard_map/all_to_all | solution.py:624
  (82 shorter events, 38.3 us)
Async XLA Ops:
  5.1 9.9 %collective-permute-start.2 = (bf16[136,384]{1,0:T(8,128)(2,1)S(1)}, bf16[136,384]{1,0:T(8,128)(2,1)S(1)}, u32[]{:S(2)}, u32[]{:S(2)}) collective-permute-start(bf16[136,384]{1,0:T(8,128)(2,1)S(1)} %get-tuple-element.76), channel_id=1, source_target_pairs={{0,48},{16,64},{32,80},{48,96},{64,112},{80,0},{96,16},{112,32},{1... | collective-permute-start | bytes 313352 | tf_op jit(solution)/shard_map/ppermute | solution.py:62
  7.3 9.0 %collective-permute-start.3 = (bf16[136,384]{1,0:T(8,128)(2,1)S(1)}, bf16[136,384]{1,0:T(8,128)(2,1)S(1)}, u32[]{:S(2)}, u32[]{:S(2)}) collective-permute-start(bf16[136,384]{1,0:T(8,128)(2,1)S(1)} %get-tuple-element.77), channel_id=1, source_target_pairs={{0,64},{16,80},{32,96},{48,112},{64,0},{80,16},{96,32},{112,48},{1... | collective-permute-start | bytes 313352 | tf_op jit(solution)/shard_map/ppermute | solution.py:62
  9.1 14.9 %collective-permute-start.13 = (bf16[128,512]{1,0:T(8,128)(2,1)S(1)}, bf16[128,512]{1,0:T(8,128)(2,1)S(1)}, u32[]{:S(2)}, u32[]{:S(2)}) collective-permute-start(bf16[128,512]{1,0:T(8,128)(2,1)S(1)} %get-tuple-element.96), channel_id=1, source_target_pairs={{0,16},{16,32},{32,48},{48,64},{64,80},{80,96},{96,112},{112,0},{1... | collective-permute-start | bytes 393224 | tf_op jit(solution)/shard_map/ppermute | solution.py:62
  9.1 15.2 %collective-permute-start.14 = (bf16[128,512]{1,0:T(8,128)(2,1)S(1)}, bf16[128,512]{1,0:T(8,128)(2,1)S(1)}, u32[]{:S(2)}, u32[]{:S(2)}) collective-permute-start(bf16[128,512]{1,0:T(8,128)(2,1)S(1)} %get-tuple-element.97), channel_id=1, source_target_pairs={{0,32},{16,48},{32,64},{48,80},{64,96},{80,112},{96,0},{112,16},{1... | collective-permute-start | bytes 393224 | tf_op jit(solution)/shard_map/ppermute | solution.py:62
  18.0 10.6 %collective-permute-start.15 = (bf16[128,512]{1,0:T(8,128)(2,1)S(1)}, bf16[128,512]{1,0:T(8,128)(2,1)S(1)}, u32[]{:S(2)}, u32[]{:S(2)}) collective-permute-start(bf16[128,512]{1,0:T(8,128)(2,1)S(1)} %get-tuple-element.98), channel_id=1, source_target_pairs={{0,48},{16,64},{32,80},{48,96},{64,112},{80,0},{96,16},{112,32},{1... | collective-permute-start | bytes 393224 | tf_op jit(solution)/shard_map/ppermute | solution.py:62
  19.7 11.7 %collective-permute-start.16 = (bf16[128,512]{1,0:T(8,128)(2,1)S(1)}, bf16[128,512]{1,0:T(8,128)(2,1)S(1)}, u32[]{:S(2)}, u32[]{:S(2)}) collective-permute-start(bf16[128,512]{1,0:T(8,128)(2,1)S(1)} %get-tuple-element.99), channel_id=1, source_target_pairs={{0,64},{16,80},{32,96},{48,112},{64,0},{80,16},{96,32},{112,48},{1... | collective-permute-start | bytes 393224 | tf_op jit(solution)/shard_map/ppermute | solution.py:62
  21.2 10.1 %collective-permute-start.17 = (bf16[128,512]{1,0:T(8,128)(2,1)S(1)}, bf16[128,512]{1,0:T(8,128)(2,1)S(1)}, u32[]{:S(2)}, u32[]{:S(2)}) collective-permute-start(bf16[128,512]{1,0:T(8,128)(2,1)S(1)} %get-tuple-element.100), channel_id=1, source_target_pairs={{0,80},{16,96},{32,112},{48,0},{64,16},{80,32},{96,48},{112,64},{1... | collective-permute-start | bytes 393224 | tf_op jit(solution)/shard_map/ppermute | solution.py:62
  24.0 10.6 %collective-permute-start.18 = (bf16[128,512]{1,0:T(8,128)(2,1)S(1)}, bf16[128,512]{1,0:T(8,128)(2,1)S(1)}, u32[]{:S(2)}, u32[]{:S(2)}) collective-permute-start(bf16[128,512]{1,0:T(8,128)(2,1)S(1)} %get-tuple-element.101), channel_id=1, source_target_pairs={{0,96},{16,112},{32,0},{48,16},{64,32},{80,48},{96,64},{112,80},{1... | collective-permute-start | bytes 393224 | tf_op jit(solution)/shard_map/ppermute | solution.py:62
  24.3 10.3 %collective-permute-start.19 = (bf16[128,512]{1,0:T(8,128)(2,1)S(1)}, bf16[128,512]{1,0:T(8,128)(2,1)S(1)}, u32[]{:S(2)}, u32[]{:S(2)}) collective-permute-start(bf16[128,512]{1,0:T(8,128)(2,1)S(1)} %get-tuple-element.102), channel_id=1, source_target_pairs={{0,112},{16,0},{32,16},{48,32},{64,48},{80,64},{96,80},{112,96},{1... | collective-permute-start | bytes 393224 | tf_op jit(solution)/shard_map/ppermute | solution.py:62
  28.5 10.1 %collective-permute-start.7 = (bf16[256,384]{1,0:T(8,128)(2,1)S(1)}, bf16[256,384]{1,0:T(8,128)(2,1)S(1)}, u32[]{:S(2)}, u32[]{:S(2)}) collective-permute-start(bf16[256,384]{1,0:T(8,128)(2,1)S(1)} %get-tuple-element.81.refs_0_), channel_id=1, source_target_pairs={{0,3},{1,0},{2,1},{3,2},{4,7},{5,4},{6,5},{7,6},{8,11},{9,8},{10,9... | collective-permute-start | bytes 589832 | tf_op jit(solution)/shard_map/ppermute | solution.py:62
  31.4 12.2 %collective-permute-start.9 = (bf16[256,384]{1,0:T(8,128)(2,1)S(1)}, bf16[256,384]{1,0:T(8,128)(2,1)S(1)}, u32[]{:S(2)}, u32[]{:S(2)}) collective-permute-start(bf16[256,384]{1,0:T(8,128)(2,1)S(1)} %get-tuple-element.81.refs_0_), channel_id=1, source_target_pairs={{0,1},{1,2},{2,3},{3,0},{4,5},{5,6},{6,7},{7,4},{8,9},{9,10},{10,1... | collective-permute-start | bytes 589832 | tf_op jit(solution)/shard_map/ppermute | solution.py:62
  35.3 10.2 %collective-permute-start.21 = (bf16[256,512]{1,0:T(8,128)(2,1)S(1)}, bf16[256,512]{1,0:T(8,128)(2,1)S(1)}, u32[]{:S(2)}, u32[]{:S(2)}) collective-permute-start(bf16[256,512]{1,0:T(8,128)(2,1)S(1)} %get-tuple-element.105.refs_1_), channel_id=1, source_target_pairs={{0,3},{1,0},{2,1},{3,2},{4,7},{5,4},{6,5},{7,6},{8,11},{9,8},{10,9... | collective-permute-start | bytes 786440 | tf_op jit(solution)/shard_map/ppermute | solution.py:62
  38.7 17.6 %collective-permute-start.22 = (bf16[256,512]{1,0:T(8,128)(2,1)S(1)}, bf16[256,512]{1,0:T(8,128)(2,1)S(1)}, u32[]{:S(2)}, u32[]{:S(2)}) collective-permute-start(bf16[256,512]{1,0:T(8,128)(2,1)S(1)} %get-tuple-element.104.refs_0_), channel_id=1, source_target_pairs={{0,1},{1,2},{2,3},{3,0},{4,5},{5,6},{6,7},{7,4},{8,9},{9,10},{10,1... | collective-permute-start | bytes 786440 | tf_op jit(solution)/shard_map/ppermute | solution.py:62
  39.9 22.5 %collective-permute-start.20 = (bf16[256,512]{1,0:T(8,128)(2,1)S(1)}, bf16[256,512]{1,0:T(8,128)(2,1)S(1)}, u32[]{:S(2)}, u32[]{:S(2)}) collective-permute-start(bf16[256,512]{1,0:T(8,128)(2,1)S(1)} %get-tuple-element.104.refs_0_), channel_id=1, source_target_pairs={{0,3},{1,0},{2,1},{3,2},{4,7},{5,4},{6,5},{7,6},{8,11},{9,8},{10,9... | collective-permute-start | bytes 786440 | tf_op jit(solution)/shard_map/ppermute | solution.py:62
  43.6 18.8 %collective-permute-start.23 = (bf16[256,512]{1,0:T(8,128)(2,1)S(1)}, bf16[256,512]{1,0:T(8,128)(2,1)S(1)}, u32[]{:S(2)}, u32[]{:S(2)}) collective-permute-start(bf16[256,512]{1,0:T(8,128)(2,1)S(1)} %get-tuple-element.105.refs_1_), channel_id=1, source_target_pairs={{0,1},{1,2},{2,3},{3,0},{4,5},{5,6},{6,7},{7,4},{8,9},{9,10},{10,1... | collective-permute-start | bytes 786440 | tf_op jit(solution)/shard_map/ppermute | solution.py:62
  43.6 15.4 %collective-permute-start.11 = (bf16[256,384]{1,0:T(8,128)(2,1)S(1)}, bf16[256,384]{1,0:T(8,128)(2,1)S(1)}, u32[]{:S(2)}, u32[]{:S(2)}) collective-permute-start(bf16[256,384]{1,0:T(8,128)(2,1)S(1)} %collective-permute-done.9.refs_4_), channel_id=1, source_target_pairs={{0,1},{1,2},{2,3},{3,0},{4,5},{5,6},{6,7},{7,4},{8,9},{9,10},{10,1... | collective-permute-start | bytes 589832 | tf_op jit(solution)/shard_map/ppermute | solution.py:62
  45.5 14.1 %collective-permute-start.12 = (bf16[256,384]{1,0:T(8,128)(2,1)S(1)}, bf16[256,384]{1,0:T(8,128)(2,1)S(1)}, u32[]{:S(2)}, u32[]{:S(2)}) collective-permute-start(bf16[256,384]{1,0:T(8,128)(2,1)S(1)} %collective-permute-done.8.refs_3_), channel_id=1, source_target_pairs={{0,3},{1,0},{2,1},{3,2},{4,7},{5,4},{6,5},{7,6},{8,11},{9,8},{10,9... | collective-permute-start | bytes 589832 | tf_op jit(solution)/shard_map/ppermute | solution.py:62
  56.3 9.7 %collective-permute-start.24 = (bf16[256,512]{1,0:T(8,128)(2,1)S(1)}, bf16[256,512]{1,0:T(8,128)(2,1)S(1)}, u32[]{:S(2)}, u32[]{:S(2)}) collective-permute-start(bf16[256,512]{1,0:T(8,128)(2,1)S(1)} %collective-permute-done.22.refs_4_), channel_id=1, source_target_pairs={{0,1},{1,2},{2,3},{3,0},{4,5},{5,6},{6,7},{7,4},{8,9},{9,10},{10,1... | collective-permute-start | bytes 786440 | tf_op jit(solution)/shard_map/ppermute | solution.py:62
  71.2 14.7 %collective-permute-start.28 = (bf16[64,3584]{1,0:T(8,128)(2,1)S(1)}, bf16[64,3584]{1,0:T(8,128)(2,1)S(1)}, u32[]{:S(2)}, u32[]{:S(2)}) collective-permute-start(bf16[64,3584]{1,0:T(8,128)(2,1)S(1)} %get-tuple-element.131), channel_id=1, source_target_pairs={{0,1},{1,2},{2,3},{3,0},{4,5},{5,6},{6,7},{7,4},{8,9},{9,10},{10,1... | collective-permute-start | bytes 1376264 | tf_op jit(solution)/shard_map/ppermute | solution.py:62
  71.3 14.6 %collective-permute-start.29 = (bf16[64,3584]{1,0:T(8,128)(2,1)S(1)}, bf16[64,3584]{1,0:T(8,128)(2,1)S(1)}, u32[]{:S(2)}, u32[]{:S(2)}) collective-permute-start(bf16[64,3584]{1,0:T(8,128)(2,1)S(1)} %get-tuple-element.133), channel_id=1, source_target_pairs={{0,3},{1,0},{2,1},{3,2},{4,7},{5,4},{6,5},{7,6},{8,11},{9,8},{10,9... | collective-permute-start | bytes 1376264 | tf_op jit(solution)/shard_map/ppermute | solution.py:62
  78.2 29.1 %collective-permute-start.26 = (bf16[64,3584]{1,0:T(8,128)(2,1)S(1)}, bf16[64,3584]{1,0:T(8,128)(2,1)S(1)}, u32[]{:S(2)}, u32[]{:S(2)}) collective-permute-start(bf16[64,3584]{1,0:T(8,128)(2,1)S(1)} %get-tuple-element.124), channel_id=1, source_target_pairs={{0,3},{1,0},{2,1},{3,2},{4,7},{5,4},{6,5},{7,6},{8,11},{9,8},{10,9... | collective-permute-start | bytes 1376264 | tf_op jit(solution)/shard_map/ppermute | solution.py:62
  78.5 28.8 %collective-permute-start.27 = (bf16[64,3584]{1,0:T(8,128)(2,1)S(1)}, bf16[64,3584]{1,0:T(8,128)(2,1)S(1)}, u32[]{:S(2)}, u32[]{:S(2)}) collective-permute-start(bf16[64,3584]{1,0:T(8,128)(2,1)S(1)} %get-tuple-element.126), channel_id=1, source_target_pairs={{0,1},{1,2},{2,3},{3,0},{4,5},{5,6},{6,7},{7,4},{8,9},{9,10},{10,1... | collective-permute-start | bytes 1376264 | tf_op jit(solution)/shard_map/ppermute | solution.py:62
  86.1 21.8 %collective-permute-start.30 = (bf16[64,3584]{1,0:T(8,128)(2,1)S(1)}, bf16[64,3584]{1,0:T(8,128)(2,1)S(1)}, u32[]{:S(2)}, u32[]{:S(2)}) collective-permute-start(bf16[64,3584]{1,0:T(8,128)(2,1)S(1)} %get-tuple-element.134), channel_id=1, source_target_pairs={{0,1},{1,2},{2,3},{3,0},{4,5},{5,6},{6,7},{7,4},{8,9},{9,10},{10,1... | collective-permute-start | bytes 1376264 | tf_op jit(solution)/shard_map/ppermute | solution.py:62
  86.4 21.5 %collective-permute-start.31 = (bf16[64,3584]{1,0:T(8,128)(2,1)S(1)}, bf16[64,3584]{1,0:T(8,128)(2,1)S(1)}, u32[]{:S(2)}, u32[]{:S(2)}) collective-permute-start(bf16[64,3584]{1,0:T(8,128)(2,1)S(1)} %get-tuple-element.135), channel_id=1, source_target_pairs={{0,3},{1,0},{2,1},{3,2},{4,7},{5,4},{6,5},{7,6},{8,11},{9,8},{10,9... | collective-permute-start | bytes 1376264 | tf_op jit(solution)/shard_map/ppermute | solution.py:62
  (17 other events, 257.2 us)

commit v2 on v1

--- a/solution.py
+++ b/solution.py
@@ -2,6 +2,7 @@
 
 import jax
 import jax.numpy as jnp
+import numpy as np
 from jax import lax
 from jax.experimental import pallas as pl
 from jax.experimental.pallas import tpu as pltpu
@@ -17,6 +18,7 @@
 PACK = 512
 ROW_COL = ("row", "col")
 ROW_COL_MP = ("row", "col", "mp")
+PARTNERS = ((2, 0), (2, 1), (1, 0), (3, 0), (1, 1), (3, 1), (0, 1))
 CHUNKS = (384, 512)
 STARTS = (0, 384)
 
@@ -54,6 +56,11 @@
     return pltpu.with_memory_space_constraint(value, pltpu.HBM)
 
 
+def across(value, chips, other):
+    pairs = [(2 * y + c, 2 * ((y + chips) % 4) + (c ^ other)) for y in range(4) for c in range(2)]
+    return lax.ppermute(value, "row", pairs)
+
+
 def in_vmem(value):
     return pltpu.with_memory_space_constraint(value, pltpu.VMEM)
 
@@ -86,18 +93,30 @@
     for load in loads:
         load.wait()
     dest_of, length_of, offset_of, group_of, reward_of, old_logp = held
+    chip, core = lax.shift_right_logical(row, 1), lax.rem(row, 2)
     for slot in range(ROWS):
-        order[lax.rem(lax.shift_right_logical(dest_of[slot], 2) - row + ROWS, ROWS)] = slot
+        to = lax.shift_right_logical(dest_of[slot], 2)
+        chips = lax.rem(lax.shift_right_logical(to, 1) - chip + 4, 4)
+        order[2 * chips + lax.rem(lax.rem(to, 2) + core, 2)] = slot
     copies = []
+    targets = [[(outs[k], 0) for k in range(ROWS)]]
+    own, near, other = outs[ROWS:]
+    targets.append(
+        [
+            (own, 0) if k == 0 else (other, k // 2) if k % 2 else (near, k // 2 - 1)
+            for k in range(ROWS)
+        ]
+    )
     for c in range(len(CHUNKS)):
         for k in range(ROWS):
+            target, at = targets[c][k]
             copies.append(
                 pltpu.make_async_copy(
                     hidden.at[
                         pl.ds(pl.multiple_of(order[k] * SLOT, SLOT), SLOT),
                         pl.ds(STARTS[c], CHUNKS[c]),
                     ],
-                    outs[c * ROWS + k].at[pl.ds(0, SLOT), :],
+                    target.at[pl.ds(at * SLOT, SLOT), :],
                     sems.at[c * ROWS + k],
                 )
             )
@@ -132,7 +151,8 @@
 
 
 def send_blocks(*args):
-    outs = [shape(SLOT + (8 if c == 0 else 0), CHUNKS[c]) for c in range(len(CHUNKS)) for _ in range(ROWS)]
+    outs = [shape(SLOT + 8, CHUNKS[0])] * ROWS
+    outs += [shape(n * SLOT, CHUNKS[1]) for n in (1, 3, 4)]
     flat = call(
         send_kernel,
         outs,
@@ -146,39 +166,51 @@
             pltpu.VMEM((ROWS, SLOT), F32),
             pltpu.SMEM((ROWS,), jnp.int32),
             pltpu.SemaphoreType.DMA((6,)),
-            pltpu.SemaphoreType.DMA((len(outs),)),
+            pltpu.SemaphoreType.DMA((2 * ROWS,)),
         ],
     )
-    return [flat[c * ROWS : (c + 1) * ROWS] for c in range(len(CHUNKS))]
-
-
-def fetch_kernel(*refs):
-    count = (len(refs) - 1) // 2
-    copies = [pltpu.make_async_copy(refs[i], refs[count + i], refs[-1].at[i]) for i in range(count)]
+    return flat[:ROWS], flat[ROWS:]
+
+
+def merge_kernel(near, other, *outs):
+    for n, out in enumerate(outs):
+        out[0:SLOT, :] = near[n * SLOT : (n + 1) * SLOT, :]
+        out[SLOT:, :] = other[(n + 1) * SLOT : (n + 2) * SLOT, :]
+
+
+def settle_kernel(positions, frequency, *refs):
+    count = (len(refs) - 3) // 2
+    cosine, sine, *held = refs[count:-1]
+    copies = [pltpu.make_async_copy(refs[i], held[i], refs[-1].at[i]) for i in range(count)]
     for copy in copies:
         copy.start()
+    angle = positions[...] * frequency[...]
+    lane = lax.broadcasted_iota(jnp.int32, angle.shape, 1)
+    cosine[...] = jnp.cos(angle)
+    sine[...] = jnp.where(lane < HEAD // 2, -1.0, 1.0) * jnp.sin(angle)
     for copy in copies:
         copy.wait()
 
 
-def fetch(*values):
+def settle(positions, frequency, *values):
     return call(
-        fetch_kernel,
-        [pltpu.VMEM(v.shape, v.dtype) for v in values],
-        [HBM] * len(values),
-        [in_hbm(v) for v in values],
-        flops=1000,
-        size=8 << 20,
+        settle_kernel,
+        [shape(PACK, HEAD, dtype=F32)] * 2 + [pltpu.VMEM(v.shape, v.dtype) for v in values],
+        [VMEM] * 2 + [HBM] * len(values),
+        [positions, frequency, *[in_hbm(v) for v in values]],
+        flops=1000000,
+        size=16 << 20,
         scratch=[pltpu.SemaphoreType.DMA((len(values),))],
     )
 
 
 def pack_kernel(first, *refs):
-    blocks = refs[:ROWS]
     if first:
+        blocks = refs[:ROWS]
         upper, lower, positions, notes = refs[ROWS:]
     else:
-        notes, upper, lower = refs[ROWS:]
+        own, other, *pairs, notes, upper, lower = refs
+        blocks = [own, other, *pairs]
     place = lax.broadcasted_iota(jnp.int32, (PACK, SLOT), 0).astype(F32)
     lane = lax.broadcasted_iota(jnp.int32, (PACK, SLOT), 1).astype(F32)
     picks = []
@@ -196,7 +228,10 @@
         if first:
             within = within + jnp.where(hit, lane, 0.0)
     pick = jnp.concatenate(picks, 1)
-    rows = jnp.concatenate([b[0:SLOT, :] for b in blocks], 0)
+    if first:
+        rows = jnp.concatenate([b[0:SLOT, :] for b in blocks], 0)
+    else:
+        rows = jnp.concatenate([own[...], other[0:SLOT, :], *[p[...] for p in pairs]], 0)
     packed = jnp.dot(pick, rows, preferred_element_type=F32).astype(BF16)
     upper[...] = packed[: PACK // 2]
     lower[...] = packed[PACK // 2 :]
@@ -205,8 +240,8 @@
 
 
 def pack(c, blocks, notes=None):
-    outs = [shape(PACK // 2, CHUNKS[c]), shape(PACK // 2, CHUNKS[c])]
     args = list(blocks)
+    outs = [shape(PACK // 2, CHUNKS[c])] * 2
     if notes is None:
         outs += [shape(PACK, SLOT, dtype=F32), shape(8 * ROWS, 2 * SLOT)]
     else:
@@ -223,8 +258,8 @@
 
 def gather_halves(upper, lower):
     left_upper = shift(upper, "mp", SHARDS, 1)
+    left_lower = shift(lower, "mp", SHARDS, 1)
     right_lower = shift(lower, "mp", SHARDS, -1)
-    left_lower = shift(lower, "mp", SHARDS, 1)
     right_upper = shift(upper, "mp", SHARDS, -1)
     far_upper = shift(left_upper, "mp", SHARDS, 1)
     far_lower = shift(right_lower, "mp", SHARDS, -1)
@@ -239,12 +274,13 @@
 def project_kernel(c, steps, carried, last, *refs):
     width = CHUNKS[c]
     refs = list(refs)
+    half = PACK // 2
     halves = [(refs.pop(0), refs.pop(0)) for _ in steps]
-    gain, w_query, w_key, w_value = [refs.pop(0) for _ in range(4)]
+    vector, w_query, w_key, w_value = [refs.pop(0) for _ in range(4)]
     if carried:
         total_in, square_in = refs.pop(0), refs.pop(0)
     if last:
-        bias, cosine, sine = refs.pop(0), refs.pop(0), refs.pop(0)
+        cosine, sine = refs.pop(0), refs.pop(0)
         queries, keys, values = refs.pop(0), refs.pop(0), refs.pop(0)
     else:
         total_out, square_out = refs.pop(0), refs.pop(0)
@@ -255,9 +291,8 @@
         own[i][...] = jnp.where(
             me < 2, upper[pl.ds(begin, SLOT), :], lower[pl.ds(begin, SLOT), :]
         )
-    half = PACK // 2
     sources = [lax.rem(me + step, SHARDS) for step in steps]
-    features = gain.shape[1]
+    features = w_query.shape[0] // SHARDS
     picked = [
         pl.ds(pl.multiple_of(source * features + STARTS[c], SLOT), width) for source in sources
     ]
@@ -277,13 +312,14 @@
             wide = pair[h][...].astype(F32)
             for j in range(0, width, SLOT):
                 square = square + wide[:, j : j + SLOT] * wide[:, j : j + SLOT]
-            factor = gain[pl.ds(sources[i], 1), STARTS[c] : STARTS[c] + width]
+            factor = vector[0:1, picked[i]]
             scaled.append((wide * factor).astype(BF16))
         if carried:
             square = square + square_in[rows, :]
         if last:
             mean = jnp.sum(square, 1, keepdims=True) * (1.0 / (SHARDS * features))
             inverse = lax.rsqrt(mean + norm_eps)
+            bias = vector[0:1, SHARDS * features :]
         else:
             square_out[rows, :] = square
         for tile in range(5):
@@ -297,7 +333,7 @@
             if not last:
                 total_out[rows, columns] = part
                 continue
-            part = part * inverse + bias[0:1, columns]
+            part = part * inverse + bias[:, columns]
             for n in range(part.shape[1] // HEAD):
                 head = part[:, n * HEAD : (n + 1) * HEAD]
                 at = 2 * tile + n
@@ -328,7 +364,8 @@
     keep = len(outs)
     outs += [shape(SLOT, width)] * len(steps)
     result = call(
-        functools.partial(project_kernel, c, steps, carried is not None, tables is not None),
+        functools.partial(
+            project_kernel, c, steps, carried is not None, tables is not None),
         outs,
         [VMEM] * len(args),
         args,
@@ -363,7 +400,7 @@
             )
             scores = jnp.where(allowed, scores * HEAD ** (-0.5), mask_fill)
             exponent = jnp.exp(scores - jnp.max(scores, 1, keepdims=True))
-            weights = (exponent / jnp.sum(exponent, 1, keepdims=True)).astype(BF16)
+            weights = (exponent * (1.0 / jnp.sum(exponent, 1, keepdims=True))).astype(BF16)
             mixed.append(
                 jnp.dot(weights, all_values, preferred_element_type=F32).astype(BF16)
             )
@@ -520,7 +557,7 @@
     chosen_rows,
     log_normalizer,
 ):
-    sent = send_blocks(
+    blocks, later = send_blocks(
         resp_dest,
         resp_len,
         resp_offset,
@@ -529,26 +566,54 @@
         old_logp.reshape(ROWS, SLOT),
         hidden,
     )
-    received = [
-        [blocks[0]] + [shift(blocks[k], "row", ROWS, k) for k in range(1, ROWS)] for blocks in sent
-    ]
-    upper, lower, positions, notes = pack(0, received[0])
+    first_blocks = [blocks[0]] + [None] * (ROWS - 1)
+    for chips, other in PARTNERS:
+        at = 2 * chips + other
+        first_blocks[at] = across(blocks[at], chips, other)
+    own_block, near_blocks, other_blocks = later
+    from_other = across(other_blocks, 0, 1)
+    merged = call(
+        merge_kernel,
+        [shape(2 * SLOT, CHUNKS[1])] * 3,
+        [VMEM] * 2,
+        (near_blocks, from_other),
+        flops=100000,
+        size=1 << 20,
+    )
+    pairs = [None] * 3
+    for chips in (1, 3, 2):
+        pairs[chips - 1] = across(merged[chips - 1], chips, 0)
+
+    vector = jnp.concatenate([v.astype(F32) for v in (attn_gain, q_bias, k_bias, v_bias)])[None, :]
+    exponents = (np.arange(HEAD) % (HEAD // 2)) * (2.0 / HEAD)
+    frequency = jnp.asarray((rope_theta ** (-exponents))[None, :], F32)
+    first_blocks[0], vector = lax.optimization_barrier((first_blocks[0], vector))
+    upper, lower, positions, notes = pack(0, first_blocks)
     first = gather_halves(upper, lower)
-    second = gather_halves(*pack(1, received[1], notes))
-
-    gain = attn_gain.astype(F32).reshape(SHARDS, -1)
-    last_gain = final_gain[None, :]
-    bias = jnp.concatenate([q_bias, k_bias, v_bias]).astype(F32)[None, :]
-    exponents = (jnp.arange(HEAD, dtype=F32) % (HEAD // 2)) * (2.0 / HEAD)
-    angles = positions * (rope_theta ** (-exponents))[None, :]
-    sign = jnp.where(jnp.arange(HEAD) < HEAD // 2, -1.0, 1.0)
-    cosine, sine = jnp.cos(angles), jnp.sin(angles) * sign[None, :]
-    gain, last_gain, bias, cosine, sine, w_query, w_key, w_value, w_out = lax.optimization_barrier(
-        (gain, last_gain, bias, cosine, sine, w_query, w_key, w_value, w_out)
-    )
-    tables = (bias, cosine, sine)
-    weights = (gain, *[in_vmem(w) for w in fetch(w_query, w_key, w_value)])
-    w_out = in_vmem(fetch(w_out)[0])
+    second = gather_halves(*pack(1, [own_block, from_other, *pairs], notes))
+    cosine, sine, *held = settle(positions, frequency, w_query, w_key, w_value, w_out)
+    *weights, w_out = [in_vmem(v) for v in held]
+    weights = (vector, *weights)
+    tables = (cosine, sine)
+    carried, own_first = project(0, (0, 1, 3, 2), first, weights)
+    carried, own_near = project(1, (0, 1, 3), second, weights, carried)
+    (queries, keys, values), own_far = project(1, (2,), second, weights, carried, tables)
+
+    attend_to = functools.partial(
+        attend,
+        queries=queries,
+        keys=keys,
+        values=values,
+        positions=positions,
+        w_out=w_out,
+    )
+    far_a, far_b = attend_to((2,))
+    from_left = shift(far_a, "mp", SHARDS, 1)
+    from_right = shift(far_b, "mp", SHARDS, -1)
+    right_a, right_b, left_a, left_b = attend_to((1, 3))
+    raw_b = shift(right_b, "mp", SHARDS, 1)
+    raw_a = shift(left_a, "mp", SHARDS, -1)
+    notes, left_b = lax.optimization_barrier((notes, left_b))
     stats, mine = call(
         sort_kernel,
         [shape(ROWS, SLOT, dtype=F32), shape(ROWS, 2 * SLOT, dtype=F32)],
@@ -557,27 +622,6 @@
         flops=100000,
         size=1 << 17,
     )
-
-    carried, own_first = project(0, (0, 1, 3, 2), first, weights)
-    carried, own_near = project(1, (0, 1, 3), second, weights, carried)
-    (queries, keys, values), own_far = project(1, (2,), second, weights, carried, tables)
-
-    attend_to = functools.partial(
-        attend,
-        queries=queries,
-        keys=keys,
-        values=values,
-        positions=positions,
-        w_out=w_out,
-    )
-    far_a, far_b = attend_to((2,))
-    from_left = shift(far_a, "mp", SHARDS, 1)
-    from_right = shift(far_b, "mp", SHARDS, -1)
-    right_a, right_b, left_a, left_b = attend_to((1, 3))
-    raw_b = shift(right_b, "mp", SHARDS, 1)
-    raw_a = shift(left_a, "mp", SHARDS, -1)
-    own_a, own_b = attend_to((0,))
-    stats, own_a = lax.optimization_barrier((stats, own_a))
     base, adv, occupied, scale = call(
         note_kernel,
         [shape(SLOT, 1, dtype=F32)] * 3 + [shape(1, 1, dtype=F32)],
@@ -601,6 +645,9 @@
     )
     two_a = shift(sum_a, "mp", SHARDS, 1)
     two_b = shift(sum_b, "mp", SHARDS, -1)
+    own_a, own_b = attend_to((0,))
+    final_gain, own_a = lax.optimization_barrier((final_gain, own_a))
+    last_gain = final_gain[None, :]
 
     own = {(0, s): v for s, v in own_first.items()}
     own |= {(1, s): v for s, v in (own_near | own_far).items()}

time: 129 us -> 125 us (0.969)
  starting transfers between devices: 50.7 us -> 47.6 us
  blocking collectives: 16.1 us -> 18.2 us
  waiting for transfers between devices: 28.3 us -> 26.6 us
    ppermute x35 -> x21, starting transfers between devices: 50.7 us -> 31.2 us  [shift(): lax.ppermute(value, axis, [(i, (i + by) % size) for i in range(size)])]
    ppermute x0 -> x11, starting transfers between devices: none -> 16.5 us  [across(): return lax.ppermute(value, 'row', pairs)]
    ppermute x35 -> x21, waiting for transfers between devices: 28.3 us -> 17.1 us  [shift(): lax.ppermute(value, axis, [(i, (i + by) % size) for i in range(size)])]
    ppermute x0 -> x11, waiting for transfers between devices: none -> 9.58 us  [across(): return lax.ppermute(value, 'row', pairs)]
    all_to_all x1, blocking collectives: 16.1 us -> 18.2 us  [body(): sums = lax.all_to_all(totals, ROW_COL_MP, 0, 0, tiled=True)]
  transfers between devices with their start and end apart: 35 -> 32, of which waited for: 14 -> 15; matrix products, arithmetic and copies ran while one was open for 1% -> 1% of each run, Pallas kernels for 16% -> 16%
where the time goes in v2:
time: 125 us; the launch traced here: 124 us
  starting transfers between devices  47.6 us (38%)
  Pallas kernels  26.6 us (21%)
  waiting for transfers between devices  26.6 us (21%)
  blocking collectives  18.2 us (15%)
  between operations  3.27 us (3%)
  other arithmetic  1.51 us (1%)
    ppermute x21, starting transfers between devices, shift(): lax.ppermute(value, axis, [(i, (i + by) % size) for i in range(size)])  31.2 us
    pallas_call x16, Pallas kernels, call(): pl.pallas_call(kernel, out_shape=out_shape, in_specs=in_specs, out_specs=...  26.6 us
    all_to_all x1, blocking collectives, body(): sums = lax.all_to_all(totals, ROW_COL_MP, 0, 0, tiled=True)  18.2 us
    ppermute x21, waiting for transfers between devices, shift(): lax.ppermute(value, axis, [(i, (i + by) % size) for i in range(size)])  17.1 us
    ppermute x11, starting transfers between devices, across(): return lax.ppermute(value, 'row', pairs)  16.5 us
    ppermute x11, waiting for transfers between devices, across(): return lax.ppermute(value, 'row', pairs)  9.58 us
  transfers between devices with their start and end apart: 32, of which 15 were waited for; matrix products, arithmetic and copies ran while one was open for 1% of the time, Pallas kernels for 16%

profile of v2, /device:TPU:0, one launch (start us, length us, event | category | flops | bytes accessed | tf_op | source)
XLA Modules:
  0.0 124.0 jit_solution(12704301335527311342)
XLA Ops:
  0.6 2.5 %shard_map.194 = (bf16[136,384]{1,0:T(8,128)(2,1)S(1)}, bf16[136,384]{1,0:T(8,128)(2,1)S(1)}, bf16[136,384]{1,0:T(8,128)(2,1)S(1)}, bf16[136,384]{1,0:T(8,128)(2...) custom-call(s32[8]{0:T(128)} %refs_0_.2, ...), custom_call_target="tpu_custom_call" | custom-call | flops 1000000 | bytes 4194304 | tf_op jit(solution)/shard_map/pallas_call | solution.py:40
  10.5 2.2 %collective-permute-start.5 = (bf16[136,384]{1,0:T(8,128)(2,1)S(1)}, bf16[136,384]{1,0:T(8,128)(2,1)S(1)}, u32[]{:S(2)}, u32[]{:S(2)}) collective-permute-start(bf16[136,384]{1,0:T(8,128)(2,1)S(1)} %get-tuple-element.76), channel_id=1, source_target_pairs={{0,96},{16,112},{32,0},{48,16},{64,32},{80,48},{96,64},{112,80},{1... | collective-permute-start | bytes 313352 | tf_op jit(solution)/shard_map/ppermute | solution.py:61
  12.7 2.0 %collective-permute-start.6 = (bf16[136,384]{1,0:T(8,128)(2,1)S(1)}, bf16[136,384]{1,0:T(8,128)(2,1)S(1)}, u32[]{:S(2)}, u32[]{:S(2)}) collective-permute-start(bf16[136,384]{1,0:T(8,128)(2,1)S(1)} %get-tuple-element.77), channel_id=1, source_target_pairs={{0,112},{16,96},{32,16},{48,0},{64,48},{80,32},{96,80},{112,64},{1... | collective-permute-start | bytes 313352 | tf_op jit(solution)/shard_map/ppermute | solution.py:61
  21.4 2.7 %collective-permute-start.14 = (bf16[256,512]{1,0:T(8,128)(2,1)S(1)}, bf16[256,512]{1,0:T(8,128)(2,1)S(1)}, u32[]{:S(2)}, u32[]{:S(2)}) collective-permute-start(bf16[256,512]{1,0:T(8,128)(2,1)S(1)} %get-tuple-element.92), channel_id=1, source_target_pairs={{0,32},{16,48},{32,64},{48,80},{64,96},{80,112},{96,0},{112,16},{1... | collective-permute-start | bytes 786440 | tf_op jit(solution)/shard_map/ppermute | solution.py:61
  32.4 4.9 %collective-permute-done.15.refs_3_ = bf16[256,512]{1,0:T(8,128)(2,1)S(1)} collective-permute-done((bf16[256,512]{1,0:T(8,128)(2,1)S(1)}, bf16[256,512]{1,0:T(8,128)(2,1)S(1)}, u32[]{:S(2)}, u32[]{:S(2)}) %collective-permute-start.15) | collective-permute-done | bytes 262176 | tf_op jit(solution)/shard_map/ppermute | solution.py:61
  40.8 2.0 %collective-permute-start.18 = (bf16[256,512]{1,0:T(8,128)(2,1)S(1)}, bf16[256,512]{1,0:T(8,128)(2,1)S(1)}, u32[]{:S(2)}, u32[]{:S(2)}) collective-permute-start(bf16[256,512]{1,0:T(8,128)(2,1)S(1)} %get-tuple-element.97.refs_1_), channel_id=1, source_target_pairs={{0,3},{1,0},{2,1},{3,2},{4,7},{5,4},{6,5},{7,6},{8,11},{9,8},{10,9... | collective-permute-start | bytes 786440 | tf_op jit(solution)/shard_map/ppermute | solution.py:69
  43.9 2.4 %collective-permute-done.11.refs_6_ = bf16[256,384]{1,0:T(8,128)(2,1)S(1)} collective-permute-done((bf16[256,384]{1,0:T(8,128)(2,1)S(1)}, bf16[256,384]{1,0:T(8,128)(2,1)S(1)}, u32[]{:S(2)}, u32[]{:S(2)}) %collective-permute-start.11) | collective-permute-done | bytes 196640 | tf_op jit(solution)/shard_map/ppermute | solution.py:69
  46.6 5.2 %shard_map.196 = (f32[512,128]{1,0:T(8,128)S(1)}, f32[512,128]{1,0:T(8,128)S(1)}, bf16[3584,896]{1,0:T(8,128)(2,1)S(1)}, bf16[3584,128]{1,0:T(8,128)(2,1)S(1)}, ...) custom-call(f32[512,128]{1,0:T(8,128)S(1)} %get-tuple-element.81.positions, f32[1,128]{1,0:T(1,128)S(1)} %copy-done.1, ...), custom_call_target="tpu_custom_call" | custom-call | flops 1000000 | bytes 16777216 | tf_op jit(solution)/shard_map/pallas_call | solution.py:40
  53.1 2.1 %collective-permute-start.22 = (bf16[256,512]{1,0:T(8,128)(2,1)S(1)}, bf16[256,512]{1,0:T(8,128)(2,1)S(1)}, u32[]{:S(2)}, u32[]{:S(2)}) collective-permute-start(bf16[256,512]{1,0:T(8,128)(2,1)S(1)} %collective-permute-done.18.refs_3_), channel_id=1, source_target_pairs={{0,3},{1,0},{2,1},{3,2},{4,7},{5,4},{6,5},{7,6},{8,11},{9,8},{10,9... | collective-permute-start | bytes 786440 | tf_op jit(solution)/shard_map/ppermute | solution.py:69
  55.2 2.8 %shard_map.197 = (f32[512,1152]{1,0:T(8,128)S(1)}, f32[512,128]{1,0:T(8,128)S(1)}, bf16[128,384]{1,0:T(8,128)(2,1)S(1)}, bf16[128,384]{1,0:T(8,128)(2,1)S(1)}, b...) custom-call(bf16[256,384]{1,0:T(8,128)(2,1)S(1)} %get-tuple-element.78.refs_0_, ...), custom_call_target="tpu_custom_call" | custom-call | flops 1811939328 | bytes 9306112 | tf_op jit(solution)/shard_map/pallas_call | solution.py:40
  59.8 2.3 %shard_map.200 = (f32[512,1152]{1,0:T(8,128)S(1)}, f32[512,128]{1,0:T(8,128)S(1)}, bf16[128,512]{1,0:T(8,128)(2,1)S(1)}, bf16[128,512]{1,0:T(8,128)(2,1)S(1)}, bf16[128,512]{1,0:T(8,128)(2,1)S(1)}) custom-call(bf16[256,512]{1,0:T(8,128)(2,1)S(1)} %get-tuple-element.96.refs_0_, bf16[256,512]{1,0:T(8,128)(2,1)S(1)} %get-tuple-element.97.refs_1_, ...), custom_call_target="tpu_custom_call" | custom-call | flops 1811939328 | bytes 9306112 | tf_op jit(solution)/shard_map/pallas_call | solution.py:40
  64.0 2.1 %shard_map.205 = (bf16[64,3584]{1,0:T(8,128)(2,1)S(1)}, bf16[64,3584]{1,0:T(8,128)(2,1)S(1)}) custom-call(bf16[512,896]{1,0:T(8,128)(2,1)S(1)} %get-tuple-element.108.queries, bf16[512,128]{1,0:T(8,128)(2,1)S(1)} %get-tuple-element.109.keys, bf16[512,128]{1,0:T(8,128)(2,1)S(1)} %get-tuple-element.110.values, f32[512,128]{1,0:T(8,128)S(1)} %get-tuple-element.81.positions, ...), custom_call_target="tpu_custom_call" | custom-call | flops 939524096 | bytes 8388608 | tf_op jit(solution)/shard_map/pallas_call | solution.py:40
  66.7 2.9 %collective-permute-start.26 = (bf16[64,3584]{1,0:T(8,128)(2,1)S(1)}, bf16[64,3584]{1,0:T(8,128)(2,1)S(1)}, u32[]{:S(2)}, u32[]{:S(2)}) collective-permute-start(bf16[64,3584]{1,0:T(8,128)(2,1)S(1)} %get-tuple-element.124), channel_id=1, source_target_pairs={{0,3},{1,0},{2,1},{3,2},{4,7},{5,4},{6,5},{7,6},{8,11},{9,8},{10,9... | collective-permute-start | bytes 1376264 | tf_op jit(solution)/shard_map/ppermute | solution.py:69
  69.5 3.7 %shard_map.203 = (bf16[64,3584]{1,0:T(8,128)(2,1)S(1)}, bf16[64,3584]{1,0:T(8,128)(2,1)S(1)}, bf16[64,3584]{1,0:T(8,128)(2,1)S(1)}, bf16[64,3584]{1,0:T(8,128)(2,1)S(1)}) custom-call(bf16[512,896]{1,0:T(8,128)(2,1)S(1)} %get-tuple-element.108.queries, bf16[512,128]{1,0:T(8,128)(2,1)S(1)} %get-tuple-element.109.keys, ...), custom_call_target="tpu_custom_call" | custom-call | flops 1879048192 | bytes 8388608 | tf_op jit(solution)/shard_map/pallas_call | solution.py:40
  73.3 2.0 %collective-permute-start.23 = (bf16[64,3584]{1,0:T(8,128)(2,1)S(1)}, bf16[64,3584]{1,0:T(8,128)(2,1)S(1)}, u32[]{:S(2)}, u32[]{:S(2)}) collective-permute-start(bf16[64,3584]{1,0:T(8,128)(2,1)S(1)} %get-tuple-element.114), channel_id=1, source_target_pairs={{0,3},{1,0},{2,1},{3,2},{4,7},{5,4},{6,5},{7,6},{8,11},{9,8},{10,9... | collective-permute-start | bytes 1376264 | tf_op jit(solution)/shard_map/ppermute | solution.py:69
  75.4 4.2 %collective-permute-done.25.b = bf16[64,3584]{1,0:T(8,128)(2,1)S(1)} collective-permute-done((bf16[64,3584]{1,0:T(8,128)(2,1)S(1)}, bf16[64,3584]{1,0:T(8,128)(2,1)S(1)}, u32[]{:S(2)}, u32[]{:S(2)}) %collective-permute-start.25) | collective-permute-done | bytes 458784 | tf_op jit(solution)/shard_map/ppermute | solution.py:69
  80.7 2.1 %collective-permute-start.27 = (bf16[64,3584]{1,0:T(8,128)(2,1)S(1)}, bf16[64,3584]{1,0:T(8,128)(2,1)S(1)}, u32[]{:S(2)}, u32[]{:S(2)}) collective-permute-start(bf16[64,3584]{1,0:T(8,128)(2,1)S(1)} %get-tuple-element.125), channel_id=1, source_target_pairs={{0,1},{1,2},{2,3},{3,0},{4,5},{5,6},{6,7},{7,4},{8,9},{9,10},{10,1... | collective-permute-start | bytes 1376264 | tf_op jit(solution)/shard_map/ppermute | solution.py:69
  82.7 2.0 %collective-permute-start.28 = (bf16[64,3584]{1,0:T(8,128)(2,1)S(1)}, bf16[64,3584]{1,0:T(8,128)(2,1)S(1)}, u32[]{:S(2)}, u32[]{:S(2)}) collective-permute-start(bf16[64,3584]{1,0:T(8,128)(2,1)S(1)} %get-tuple-element.126), channel_id=1, source_target_pairs={{0,3},{1,0},{2,1},{3,2},{4,7},{5,4},{6,5},{7,6},{8,11},{9,8},{10,9... | collective-permute-start | bytes 1376264 | tf_op jit(solution)/shard_map/ppermute | solution.py:69
  84.9 2.0 %collective-permute-start.29 = (f32[8,128]{1,0:T(8,128)S(1)}, f32[8,128]{1,0:T(8,128)S(1)}, u32[]{:S(2)}, u32[]{:S(2)}) collective-permute-start(f32[8,128]{1,0:T(8,128)S(1)} %get-tuple-element.128.stats_a), channel_id=1, source_target_pairs={{0,4},{4,8},{8,12},{12,0},{1,5},{5,9},{9,13},{13,1},{2,6},{6,10},{... | collective-permute-start | bytes 12296 | tf_op jit(solution)/shard_map/ppermute | solution.py:69
  86.9 3.7 %collective-permute-done.29.stats_b = f32[8,128]{1,0:T(8,128)S(1)} collective-permute-done((f32[8,128]{1,0:T(8,128)S(1)}, f32[8,128]{1,0:T(8,128)S(1)}, u32[]{:S(2)}, u32[]{:S(2)}) %collective-permute-start.29) | collective-permute-done | bytes 4128 | tf_op jit(solution)/shard_map/ppermute | solution.py:69
  92.5 3.2 %collective-permute-done.30.stats_c = f32[8,128]{1,0:T(8,128)S(1)} collective-permute-done((f32[8,128]{1,0:T(8,128)S(1)}, f32[8,128]{1,0:T(8,128)S(1)}, u32[]{:S(2)}, u32[]{:S(2)}) %collective-permute-start.30) | collective-permute-done | bytes 4128 | tf_op jit(solution)/shard_map/ppermute | solution.py:69
  95.7 2.0 %collective-permute-start.31 = (f32[8,128]{1,0:T(8,128)S(1)}, f32[8,128]{1,0:T(8,128)S(1)}, u32[]{:S(2)}, u32[]{:S(2)}) collective-permute-start(f32[8,128]{1,0:T(8,128)S(1)} %get-tuple-element.128.stats_a), channel_id=1, source_target_pairs={{0,12},{4,0},{8,4},{12,8},{1,13},{5,1},{9,5},{13,9},{2,14},{6,2},{... | collective-permute-start | bytes 12296 | tf_op jit(solution)/shard_map/ppermute | solution.py:69
  97.7 2.1 %shard_map.202 = (bf16[64,3584]{1,0:T(8,128)(2,1)S(1)}, bf16[64,3584]{1,0:T(8,128)(2,1)S(1)}) custom-call(bf16[512,896]{1,0:T(8,128)(2,1)S(1)} %get-tuple-element.108.queries, bf16[512,128]{1,0:T(8,128)(2,1)S(1)} %get-tuple-element.109.keys, bf16[512,128]{1,0:T(8,128)(2,1)S(1)} %get-tuple-element.110.values, f32[512,128]{1,0:T(8,128)S(1)} %get-tuple-element.81.positions, ...), custom_call_target="tpu_custom_call" | custom-call | flops 939524096 | bytes 8388608 | tf_op jit(solution)/shard_map/pallas_call | solution.py:40
  102.6 18.2 %all_to_all.5 = f32[128,1,128]{2,1,0:T(1,128)S(1)} all-to-all(f32[128,1,128]{2,1,0:T(1,128)S(1)} %get-tuple-element.134), channel_id=1, replica_groups=mesh['row'=8,'col'=4,'mp'=4] {'row','col','mp'}, dimensions={0} | all-to-all | bytes 131072 | tf_op jit(solution)/shard_map/all_to_all | solution.py:671
  (69 shorter events, 39.3 us)
Async XLA Ops:
  3.2 18.1 %collective-permute-start.13 = (bf16[512,512]{1,0:T(8,128)(2,1)S(1)}, bf16[512,512]{1,0:T(8,128)(2,1)S(1)}, u32[]{:S(2)}, u32[]{:S(2)}) collective-permute-start(bf16[512,512]{1,0:T(8,128)(2,1)S(1)} %get-tuple-element.90), channel_id=1, source_target_pairs={{0,16},{16,0},{32,48},{48,32},{64,80},{80,64},{96,112},{112,96},{1... | collective-permute-start | bytes 1572872 | tf_op jit(solution)/shard_map/ppermute | solution.py:61
  6.4 10.2 %collective-permute-start.3 = (bf16[136,384]{1,0:T(8,128)(2,1)S(1)}, bf16[136,384]{1,0:T(8,128)(2,1)S(1)}, u32[]{:S(2)}, u32[]{:S(2)}) collective-permute-start(bf16[136,384]{1,0:T(8,128)(2,1)S(1)} %get-tuple-element.74), channel_id=1, source_target_pairs={{0,64},{16,80},{32,96},{48,112},{64,0},{80,16},{96,32},{112,48},{1... | collective-permute-start | bytes 313352 | tf_op jit(solution)/shard_map/ppermute | solution.py:61
  8.3 8.7 %collective-permute-start.4 = (bf16[136,384]{1,0:T(8,128)(2,1)S(1)}, bf16[136,384]{1,0:T(8,128)(2,1)S(1)}, u32[]{:S(2)}, u32[]{:S(2)}) collective-permute-start(bf16[136,384]{1,0:T(8,128)(2,1)S(1)} %get-tuple-element.75), channel_id=1, source_target_pairs={{0,80},{16,64},{32,112},{48,96},{64,16},{80,0},{96,48},{112,32},{1... | collective-permute-start | bytes 313352 | tf_op jit(solution)/shard_map/ppermute | solution.py:61
  19.7 8.8 %collective-permute-start.9 = (bf16[256,384]{1,0:T(8,128)(2,1)S(1)}, bf16[256,384]{1,0:T(8,128)(2,1)S(1)}, u32[]{:S(2)}, u32[]{:S(2)}) collective-permute-start(bf16[256,384]{1,0:T(8,128)(2,1)S(1)} %get-tuple-element.78.refs_0_), channel_id=1, source_target_pairs={{0,1},{1,2},{2,3},{3,0},{4,5},{5,6},{6,7},{7,4},{8,9},{9,10},{10,1... | collective-permute-start | bytes 589832 | tf_op jit(solution)/shard_map/ppermute | solution.py:69
  21.4 9.5 %collective-permute-start.14 = (bf16[256,512]{1,0:T(8,128)(2,1)S(1)}, bf16[256,512]{1,0:T(8,128)(2,1)S(1)}, u32[]{:S(2)}, u32[]{:S(2)}) collective-permute-start(bf16[256,512]{1,0:T(8,128)(2,1)S(1)} %get-tuple-element.92), channel_id=1, source_target_pairs={{0,32},{16,48},{32,64},{48,80},{64,96},{80,112},{96,0},{112,16},{1... | collective-permute-start | bytes 786440 | tf_op jit(solution)/shard_map/ppermute | solution.py:61
  24.1 13.3 %collective-permute-start.15 = (bf16[256,512]{1,0:T(8,128)(2,1)S(1)}, bf16[256,512]{1,0:T(8,128)(2,1)S(1)}, u32[]{:S(2)}, u32[]{:S(2)}) collective-permute-start(bf16[256,512]{1,0:T(8,128)(2,1)S(1)} %get-tuple-element.93), channel_id=1, source_target_pairs={{0,64},{16,80},{32,96},{48,112},{64,0},{80,16},{96,32},{112,48},{1... | collective-permute-start | bytes 786440 | tf_op jit(solution)/shard_map/ppermute | solution.py:61
  25.7 13.1 %collective-permute-start.16 = (bf16[256,512]{1,0:T(8,128)(2,1)S(1)}, bf16[256,512]{1,0:T(8,128)(2,1)S(1)}, u32[]{:S(2)}, u32[]{:S(2)}) collective-permute-start(bf16[256,512]{1,0:T(8,128)(2,1)S(1)} %get-tuple-element.94), channel_id=1, source_target_pairs={{0,96},{16,112},{32,0},{48,16},{64,32},{80,48},{96,64},{112,80},{1... | collective-permute-start | bytes 786440 | tf_op jit(solution)/shard_map/ppermute | solution.py:61
  26.8 14.0 %collective-permute-start.7 = (bf16[256,384]{1,0:T(8,128)(2,1)S(1)}, bf16[256,384]{1,0:T(8,128)(2,1)S(1)}, u32[]{:S(2)}, u32[]{:S(2)}) collective-permute-start(bf16[256,384]{1,0:T(8,128)(2,1)S(1)} %get-tuple-element.78.refs_0_), channel_id=1, source_target_pairs={{0,3},{1,0},{2,1},{3,2},{4,7},{5,4},{6,5},{7,6},{8,11},{9,8},{10,9... | collective-permute-start | bytes 589832 | tf_op jit(solution)/shard_map/ppermute | solution.py:69
  28.6 14.3 %collective-permute-start.8 = (bf16[256,384]{1,0:T(8,128)(2,1)S(1)}, bf16[256,384]{1,0:T(8,128)(2,1)S(1)}, u32[]{:S(2)}, u32[]{:S(2)}) collective-permute-start(bf16[256,384]{1,0:T(8,128)(2,1)S(1)} %get-tuple-element.79.refs_1_), channel_id=1, source_target_pairs={{0,3},{1,0},{2,1},{3,2},{4,7},{5,4},{6,5},{7,6},{8,11},{9,8},{10,9... | collective-permute-start | bytes 589832 | tf_op jit(solution)/shard_map/ppermute | solution.py:69
  30.9 12.5 %collective-permute-start.10 = (bf16[256,384]{1,0:T(8,128)(2,1)S(1)}, bf16[256,384]{1,0:T(8,128)(2,1)S(1)}, u32[]{:S(2)}, u32[]{:S(2)}) collective-permute-start(bf16[256,384]{1,0:T(8,128)(2,1)S(1)} %get-tuple-element.79.refs_1_), channel_id=1, source_target_pairs={{0,1},{1,2},{2,3},{3,0},{4,5},{5,6},{6,7},{7,4},{8,9},{9,10},{10,1... | collective-permute-start | bytes 589832 | tf_op jit(solution)/shard_map/ppermute | solution.py:69
  37.3 9.0 %collective-permute-start.11 = (bf16[256,384]{1,0:T(8,128)(2,1)S(1)}, bf16[256,384]{1,0:T(8,128)(2,1)S(1)}, u32[]{:S(2)}, u32[]{:S(2)}) collective-permute-start(bf16[256,384]{1,0:T(8,128)(2,1)S(1)} %collective-permute-done.9.refs_4_), channel_id=1, source_target_pairs={{0,1},{1,2},{2,3},{3,0},{4,5},{5,6},{6,7},{7,4},{8,9},{9,10},{10,1... | collective-permute-start | bytes 589832 | tf_op jit(solution)/shard_map/ppermute | solution.py:69
  39.6 12.4 %collective-permute-start.19 = (bf16[256,512]{1,0:T(8,128)(2,1)S(1)}, bf16[256,512]{1,0:T(8,128)(2,1)S(1)}, u32[]{:S(2)}, u32[]{:S(2)}) collective-permute-start(bf16[256,512]{1,0:T(8,128)(2,1)S(1)} %get-tuple-element.96.refs_0_), channel_id=1, source_target_pairs={{0,1},{1,2},{2,3},{3,0},{4,5},{5,6},{6,7},{7,4},{8,9},{9,10},{10,1... | collective-permute-start | bytes 786440 | tf_op jit(solution)/shard_map/ppermute | solution.py:69
  40.8 12.3 %collective-permute-start.18 = (bf16[256,512]{1,0:T(8,128)(2,1)S(1)}, bf16[256,512]{1,0:T(8,128)(2,1)S(1)}, u32[]{:S(2)}, u32[]{:S(2)}) collective-permute-start(bf16[256,512]{1,0:T(8,128)(2,1)S(1)} %get-tuple-element.97.refs_1_), channel_id=1, source_target_pairs={{0,3},{1,0},{2,1},{3,2},{4,7},{5,4},{6,5},{7,6},{8,11},{9,8},{10,9... | collective-permute-start | bytes 786440 | tf_op jit(solution)/shard_map/ppermute | solution.py:69
  42.9 12.3 %collective-permute-start.12 = (bf16[256,384]{1,0:T(8,128)(2,1)S(1)}, bf16[256,384]{1,0:T(8,128)(2,1)S(1)}, u32[]{:S(2)}, u32[]{:S(2)}) collective-permute-start(bf16[256,384]{1,0:T(8,128)(2,1)S(1)} %collective-permute-done.8.refs_3_), channel_id=1, source_target_pairs={{0,3},{1,0},{2,1},{3,2},{4,7},{5,4},{6,5},{7,6},{8,11},{9,8},{10,9... | collective-permute-start | bytes 589832 | tf_op jit(solution)/shard_map/ppermute | solution.py:69
  43.4 16.4 %collective-permute-start.17 = (bf16[256,512]{1,0:T(8,128)(2,1)S(1)}, bf16[256,512]{1,0:T(8,128)(2,1)S(1)}, u32[]{:S(2)}, u32[]{:S(2)}) collective-permute-start(bf16[256,512]{1,0:T(8,128)(2,1)S(1)} %get-tuple-element.96.refs_0_), channel_id=1, source_target_pairs={{0,3},{1,0},{2,1},{3,2},{4,7},{5,4},{6,5},{7,6},{8,11},{9,8},{10,9... | collective-permute-start | bytes 786440 | tf_op jit(solution)/shard_map/ppermute | solution.py:69
  46.3 13.5 %collective-permute-start.20 = (bf16[256,512]{1,0:T(8,128)(2,1)S(1)}, bf16[256,512]{1,0:T(8,128)(2,1)S(1)}, u32[]{:S(2)}, u32[]{:S(2)}) collective-permute-start(bf16[256,512]{1,0:T(8,128)(2,1)S(1)} %get-tuple-element.97.refs_1_), channel_id=1, source_target_pairs={{0,1},{1,2},{2,3},{3,0},{4,5},{5,6},{6,7},{7,4},{8,9},{9,10},{10,1... | collective-permute-start | bytes 786440 | tf_op jit(solution)/shard_map/ppermute | solution.py:69
  51.9 10.2 %collective-permute-start.21 = (bf16[256,512]{1,0:T(8,128)(2,1)S(1)}, bf16[256,512]{1,0:T(8,128)(2,1)S(1)}, u32[]{:S(2)}, u32[]{:S(2)}) collective-permute-start(bf16[256,512]{1,0:T(8,128)(2,1)S(1)} %collective-permute-done.19.refs_4_), channel_id=1, source_target_pairs={{0,1},{1,2},{2,3},{3,0},{4,5},{5,6},{6,7},{7,4},{8,9},{9,10},{10,1... | collective-permute-start | bytes 786440 | tf_op jit(solution)/shard_map/ppermute | solution.py:69
  53.1 9.8 %collective-permute-start.22 = (bf16[256,512]{1,0:T(8,128)(2,1)S(1)}, bf16[256,512]{1,0:T(8,128)(2,1)S(1)}, u32[]{:S(2)}, u32[]{:S(2)}) collective-permute-start(bf16[256,512]{1,0:T(8,128)(2,1)S(1)} %collective-permute-done.18.refs_3_), channel_id=1, source_target_pairs={{0,3},{1,0},{2,1},{3,2},{4,7},{5,4},{6,5},{7,6},{8,11},{9,8},{10,9... | collective-permute-start | bytes 786440 | tf_op jit(solution)/shard_map/ppermute | solution.py:69
  66.1 13.5 %collective-permute-start.25 = (bf16[64,3584]{1,0:T(8,128)(2,1)S(1)}, bf16[64,3584]{1,0:T(8,128)(2,1)S(1)}, u32[]{:S(2)}, u32[]{:S(2)}) collective-permute-start(bf16[64,3584]{1,0:T(8,128)(2,1)S(1)} %get-tuple-element.121), channel_id=1, source_target_pairs={{0,1},{1,2},{2,3},{3,0},{4,5},{5,6},{6,7},{7,4},{8,9},{9,10},{10,1... | collective-permute-start | bytes 1376264 | tf_op jit(solution)/shard_map/ppermute | solution.py:69
  66.7 13.8 %collective-permute-start.26 = (bf16[64,3584]{1,0:T(8,128)(2,1)S(1)}, bf16[64,3584]{1,0:T(8,128)(2,1)S(1)}, u32[]{:S(2)}, u32[]{:S(2)}) collective-permute-start(bf16[64,3584]{1,0:T(8,128)(2,1)S(1)} %get-tuple-element.124), channel_id=1, source_target_pairs={{0,3},{1,0},{2,1},{3,2},{4,7},{5,4},{6,5},{7,6},{8,11},{9,8},{10,9... | collective-permute-start | bytes 1376264 | tf_op jit(solution)/shard_map/ppermute | solution.py:69
  73.3 27.6 %collective-permute-start.23 = (bf16[64,3584]{1,0:T(8,128)(2,1)S(1)}, bf16[64,3584]{1,0:T(8,128)(2,1)S(1)}, u32[]{:S(2)}, u32[]{:S(2)}) collective-permute-start(bf16[64,3584]{1,0:T(8,128)(2,1)S(1)} %get-tuple-element.114), channel_id=1, source_target_pairs={{0,3},{1,0},{2,1},{3,2},{4,7},{5,4},{6,5},{7,6},{8,11},{9,8},{10,9... | collective-permute-start | bytes 1376264 | tf_op jit(solution)/shard_map/ppermute | solution.py:69
  75.3 25.6 %collective-permute-start.24 = (bf16[64,3584]{1,0:T(8,128)(2,1)S(1)}, bf16[64,3584]{1,0:T(8,128)(2,1)S(1)}, u32[]{:S(2)}, u32[]{:S(2)}) collective-permute-start(bf16[64,3584]{1,0:T(8,128)(2,1)S(1)} %get-tuple-element.116), channel_id=1, source_target_pairs={{0,1},{1,2},{2,3},{3,0},{4,5},{5,6},{6,7},{7,4},{8,9},{9,10},{10,1... | collective-permute-start | bytes 1376264 | tf_op jit(solution)/shard_map/ppermute | solution.py:69
  80.7 20.8 %collective-permute-start.27 = (bf16[64,3584]{1,0:T(8,128)(2,1)S(1)}, bf16[64,3584]{1,0:T(8,128)(2,1)S(1)}, u32[]{:S(2)}, u32[]{:S(2)}) collective-permute-start(bf16[64,3584]{1,0:T(8,128)(2,1)S(1)} %get-tuple-element.125), channel_id=1, source_target_pairs={{0,1},{1,2},{2,3},{3,0},{4,5},{5,6},{6,7},{7,4},{8,9},{9,10},{10,1... | collective-permute-start | bytes 1376264 | tf_op jit(solution)/shard_map/ppermute | solution.py:69
  82.7 18.7 %collective-permute-start.28 = (bf16[64,3584]{1,0:T(8,128)(2,1)S(1)}, bf16[64,3584]{1,0:T(8,128)(2,1)S(1)}, u32[]{:S(2)}, u32[]{:S(2)}) collective-permute-start(bf16[64,3584]{1,0:T(8,128)(2,1)S(1)} %get-tuple-element.126), channel_id=1, source_target_pairs={{0,3},{1,0},{2,1},{3,2},{4,7},{5,4},{6,5},{7,6},{8,11},{9,8},{10,9... | collective-permute-start | bytes 1376264 | tf_op jit(solution)/shard_map/ppermute | solution.py:69
  (12 other events, 136.2 us)
